TPU v7x, 256 devices: a whole 4x4x8 slice. The times are simulated.
256 devices in a mesh: mem: 64 (over x, z, core), chan: 4 (over y).
Axes of the slice: x: 4, y: 4, z: 8, core: 2. Of those that a mesh axis runs over, the one named last changes fastest.
Arguments:
- state_anom: bfloat16 [64, 512, 137], P(None, 'mem'), may hold values from -6 to 6
- radiance_anom: bfloat16 [64, 512, 8704], P(None, 'mem', 'chan'), may hold values from -6 to 6
- inv_noise: float32 [8704], P('chan'), may hold values from 0.02 to 0.2
- innovation: float32 [64, 8704], P(None, 'chan'), may hold values from -6 to 6
- valid_count: int32 [64], replicated, may hold values from 4352 to 8461
Outputs:
- information: float32 [64, 137, 137], P('mem')
- gradient: float32 [64, 137], P('mem')
- increment: float32 [64, 137], P('mem')
All inputs are finite; a program needn't handle non-finite values.
Results may differ from a plain program's by a relative error of at most 0.0003.
Values may be sent and summed in bfloat16 or wider, within the bound.
No kernel may reach another device: no remote copies, remote signals or barrier semaphores. Data moves between devices by JAX's collectives and lax.ppermute only.
A program may use at most 64 MiB of HBM per device.

v0:
```python
import jax
import jax.numpy as jnp
from jax import lax
from jax.sharding import PartitionSpec as P


def side_by_side(arrays, axis, split_dim, concat_dim, along):
    widths = [a.shape[along] for a in arrays]
    both = jnp.concatenate(arrays, axis=along)
    result = lax.all_to_all(both, axis, split_axis=split_dim, concat_axis=concat_dim, tiled=True)
    return tuple(jnp.split(result, [sum(widths[:k]) for k in range(1, len(widths))], axis=along))


def sent_to_all(x, axis):
    size = lax.axis_size(axis)
    return lax.all_to_all(jnp.broadcast_to(x[None], (size, *x.shape)), axis, 0, 0, tiled=True)


def over_copies(x, axis):
    return sent_to_all(x, axis).sum(axis=0)


def packed_total(arrays, axis):
    ends = [0]
    for a in arrays:
        ends.append(ends[-1] + a.size)
    subtotal = over_copies(jnp.concatenate([a.ravel() for a in arrays]), axis)
    return tuple((subtotal[b:e].reshape(a.shape) for a, b, e in zip(arrays, ends, ends[1:])))


def slab_terms(cross, weight, innov_rows):
    weighted = cross * weight[:, :, None]
    info_part = jnp.einsum("pcs,pct->pst", weighted, cross, precision=lax.Precision.HIGHEST)
    grad_part = jnp.einsum("pcs,pc->ps", weighted, innov_rows, precision=lax.Precision.HIGHEST)
    return (info_part, grad_part)


def shards(state_anom, radiance_anom, inv_noise, innovation, valid_count):
    profiles = state_anom.shape[0]
    states = state_anom.shape[2]
    slab_width = radiance_anom.shape[2]
    members_all = state_anom.shape[1] * lax.axis_size("mem")
    prof_local = profiles // lax.axis_size("mem")
    slab_start = lax.axis_index("chan") * slab_width
    own_rad, own_states = side_by_side((radiance_anom, state_anom), "mem", 0, 1, 2)
    cross = jnp.einsum("pmc,pms->pcs", own_rad, own_states, preferred_element_type=jnp.float32)
    cross = cross / jnp.float32(members_all - 1)
    first_prof = lax.axis_index("mem") * prof_local
    own_count = lax.dynamic_slice_in_dim(valid_count, first_prof, prof_local, 0)
    slots = slab_start + jnp.arange(slab_width, dtype=jnp.int32)
    valid = (slots[None, :] < own_count[:, None]).astype(jnp.float32)
    weight = inv_noise[None, :] * valid
    innov_rows = lax.dynamic_slice_in_dim(innovation, first_prof, prof_local, 0)
    info_share, grad_share = slab_terms(cross, weight, innov_rows)
    information, gradient = packed_total((info_share, grad_share), "chan")
    system = information + jnp.eye(states, dtype=jnp.float32)[None]
    factor = jnp.linalg.cholesky(system)
    increment = jax.scipy.linalg.cho_solve((factor, True), gradient[:, :, None])[:, :, 0]
    return (information, gradient, increment)


def solution(mesh):
    in_specs = (P(None, "mem", None), P(None, "mem", "chan"), P("chan"), P(None, "chan"), P())
    out_specs = (P("mem", None, None), P("mem", None), P("mem", None))
    return jax.shard_map(shards, mesh=mesh, in_specs=in_specs, out_specs=out_specs, check_vma=False)
```

profile of v0, /device:TPU:1, one launch (start us, length us, event | category | flops | bytes accessed | tf_op | source)
XLA Modules:
  0.0 140.8 jit_solution(7269212480603147473)
XLA Ops:
  0.6 3.4 %pad_maximum_fusion = bf16[64,8,2313]{2,1,0:T(8,128)(2,1)} fusion(bf16[64,8,137]{2,1,0:T(8,128)(2,1)} %param.5, bf16[64,8,2176]{2,1,0:T(8,128)(2,1)} %param.6), kind=kLoop, calls=%fused_computation | loop fusion | flops 4737024 | bytes 4737024 | tf_op jit(solution)/shard_map/concatenate | solution.py:9
  4.1 13.1 %all-to-all-start = ((bf16[64,8,2313]{2,1,0:T(8,128)(2,1)}), bf16[64,8,2313]{2,1,0:T(8,128)(2,1)S(1)}, u32[]{:S(2)}, u32[]{:S(2)}) async-start(bf16[64,8,2313]{2,1,0:T(8,128)(2,1)} %pad_maximum_fusion), calls=%async_computation | async-start | bytes 4980736 | tf_op jit(solution)/shard_map/all_to_all | solution.py:10
  17.2 0.6 dynamic_slice.6
  17.8 0.7 select_multiply_fusion
  18.4 58.2 %all-to-all-done = bf16[64,8,2313]{2,1,0:T(8,128)(2,1)S(1)} async-done(((bf16[64,8,2313]{2,1,0:T(8,128)(2,1)}), bf16[64,8,2313]{2,1,0:T(8,128)(2,1)S(1)}, u32[]{:S(2)}, u32[]{:S(2)}) %all-to-all-start) | async-done | bytes 2368544 | tf_op jit(solution)/shard_map/all_to_all | solution.py:10
  76.6 0.6 fusion
  77.1 1.3 fusion.1
  78.4 1.1 fusion.3
  79.6 0.3 reshape.221
  80.0 0.9 broadcast_in_dim.5
  80.9 4.2 %all-to-all-start.1 = ((f32[4,1,18906]{2,1,0:T(1,128)}), f32[4,1,18906]{2,1,0:T(1,128)S(1)}, u32[]{:S(2)}, u32[]{:S(2)}) async-start(f32[4,1,18906]{2,1,0:T(1,128)} %broadcast_in_dim.5), calls=%async_computation.1 | async-start | bytes 606208 | tf_op jit(solution)/shard_map/all_to_all | solution.py:16
  85.1 6.5 %all-to-all-done.1 = f32[4,1,18906]{2,1,0:T(1,128)S(1)} async-done(((f32[4,1,18906]{2,1,0:T(1,128)}), f32[4,1,18906]{2,1,0:T(1,128)S(1)}, u32[]{:S(2)}, u32[]{:S(2)}) %all-to-all-start.1) | async-done | bytes 302528 | tf_op jit(solution)/shard_map/all_to_all | solution.py:16
  91.6 0.3 reduce_sum.9
  91.9 0.6 slice.102
  92.5 0.3 reshape.223
  92.8 0.8 copy.23
  93.8 0.1 copy.21
  93.9 11.7 %custom-call.20 = f32[1,128,128]{2,1,0:T(8,128)S(1)} custom-call(f32[1,128,128]{2,1,0:T(8,128)S(1)} %cholesky.123), custom_call_target="Cholesky" | custom-call | tf_op jit(solution)/shard_map/jit(cholesky)/cholesky | solution.py:57
  105.7 9.8 %custom-call.21 = f32[1,1,128,128]{2,3,1,0:T(8,128)S(1)} custom-call(f32[1,1,128,128]{3,2,1,0:T(8,128)S(1)} %get-tuple-element.36), custom_call_target="InvertDiagBlocksLowerTriangular" | custom-call | tf_op jit(solution)/shard_map/jit(cholesky)/cholesky | solution.py:57
  115.5 0.2 bitcast_dynamic-update-slice_fusion
  115.7 0.1 fusion.6
  115.8 0.8 custom-call.22
  116.6 0.7 compare_reduce_fusion.1
  117.3 0.7 compare_reduce_fusion
  119.5 19.7 %custom-call.23 = f32[2,128,128]{1,2,0:T(8,128)S(1)} custom-call(f32[2,128,128]{2,1,0:T(8,128)S(1)} %pad_maximum_fusion.1), custom_call_target="InvertDiagBlocksLowerTriangular" | custom-call | tf_op jit(solution)/shard_map/jit(_cho_solve)/triangular_solve | solution.py:58
  139.2 0.2 fusion.18
  139.4 0.1 fusion.10
  139.5 0.2 convolution_bitcast_fusion.4
  139.7 0.1 convolution_bitcast_fusion.3
  139.8 0.1 fusion.8
  140.0 0.2 convolution_bitcast_fusion.1
  140.2 0.6 maximum_bitcast_fusion
  (20 shorter events, 0.5 us)
Async XLA Ops:
  0.6 77.8 %copy-start = (f32[64,2176]{1,0:T(8,128)S(1)}, f32[64,2176]{1,0:T(8,128)}, u32[]{:S(2)}) copy-start(f32[64,2176]{1,0:T(8,128)} %param.8) | copy-start | bytes 1671172
  4.1 13.1 %copy-start.2 = (s32[64]{0:T(128)S(1)}, s32[64]{0:T(128)}, u32[]{:S(2)}) copy-start(s32[64]{0:T(128)} %param.9) | copy-start | bytes 772
  4.1 13.7 %copy-start.1 = (f32[2176]{0:T(1024)S(1)}, f32[2176]{0:T(1024)}, u32[]{:S(2)}) copy-start(f32[2176]{0:T(1024)} %param.7) | copy-start | bytes 26116
  4.1 72.5 %all-to-all-start = ((bf16[64,8,2313]{2,1,0:T(8,128)(2,1)}), bf16[64,8,2313]{2,1,0:T(8,128)(2,1)S(1)}, u32[]{:S(2)}, u32[]{:S(2)}) async-start(bf16[64,8,2313]{2,1,0:T(8,128)(2,1)} %pad_maximum_fusion), calls=%async_computation | async-start | bytes 4980736 | tf_op jit(solution)/shard_map/all_to_all | solution.py:10
  80.9 10.7 %all-to-all-start.1 = ((f32[4,1,18906]{2,1,0:T(1,128)}), f32[4,1,18906]{2,1,0:T(1,128)S(1)}, u32[]{:S(2)}, u32[]{:S(2)}) async-start(f32[4,1,18906]{2,1,0:T(1,128)} %broadcast_in_dim.5), calls=%async_computation.1 | async-start | bytes 606208 | tf_op jit(solution)/shard_map/all_to_all | solution.py:16
where the time goes:
time: 141 us
  waiting for transfers between devices  64.6 us (46%)
  other arithmetic  48.7 us (35%)
  starting transfers between devices  17.3 us (12%)
  matrix products  4.23 us (3%)
  local copies, waits for them, and re-layouts  3.8 us (3%)
  between operations  2.16 us (2%)
    all_to_all x1, waiting for transfers between devices, side_by_side(): lax.all_to_all(both, axis, split_axis=split_dim, concat_axis=concat_dim,...  58.2 us
    another operation x7, other arithmetic, shards(): factor = jnp.linalg.cholesky(system)  23.8 us
    another operation x6, other arithmetic, shards(): jax.scipy.linalg.cho_solve((factor, True), gradient[:, :, None])[:, :, 0]  19.8 us
    all_to_all x1, starting transfers between devices, side_by_side(): lax.all_to_all(both, axis, split_axis=split_dim, concat_axis=concat_dim,...  13.1 us
    all_to_all x1, waiting for transfers between devices, sent_to_all(): lax.all_to_all(jnp.broadcast_to(x[None], (size, *x.shape)), axis, 0, 0, t...  6.48 us
    all_to_all x1, starting transfers between devices, sent_to_all(): lax.all_to_all(jnp.broadcast_to(x[None], (size, *x.shape)), axis, 0, 0, t...  4.19 us
    concatenate x1, other arithmetic, side_by_side(): both = jnp.concatenate(arrays, axis=along)  3.41 us
  transfers between devices with their start and end apart: 2, of which 2 were waited for; matrix products, arithmetic and copies ran while one was open for 1% of the time, Pallas kernels for 0%

commit v1 on v0

v1 whole, which is shorter than its diff:
```python
import functools

import jax
import jax.numpy as jnp
from jax import lax
from jax.experimental import pallas as pl
from jax.experimental.pallas import tpu as pltpu
from jax.sharding import PartitionSpec as P

LANES = 128
TOL = 1e-5
FIRST_STEPS = 10
MORE_STEPS = 4
MORE_ROUNDS = 8


def diagonal(rows):
    r = lax.broadcasted_iota(jnp.int32, (rows, LANES), 0)
    c = lax.broadcasted_iota(jnp.int32, (rows, LANES), 1)
    return r, c


def slab_kernel(states, members_all, x_ref, weight_ref, innov_ref, out_ref):
    width = weight_ref.shape[1]
    rad = x_ref[:, 0:width]
    st = x_ref[:, width : width + states]
    cross = lax.dot_general(st, rad, (((0,), (0,)), ((), ())), preferred_element_type=jnp.float32)
    root = jnp.sqrt(weight_ref[...])
    y = cross * (root * (1.0 / (members_all - 1)))
    y1 = y.astype(jnp.bfloat16)
    y2 = (y - y1.astype(jnp.float32)).astype(jnp.bfloat16)
    nt = (((1,), (1,)), ((), ()))
    main = lax.dot_general(y1, y1, nt, preferred_element_type=jnp.float32)
    side = lax.dot_general(y2, y1, nt, preferred_element_type=jnp.float32)
    info = main + (side + side.T)
    grad = jnp.sum(y * (root * innov_ref[...]), axis=1, keepdims=True)
    r = lax.broadcasted_iota(jnp.int32, info.shape, 0)
    c = lax.broadcasted_iota(jnp.int32, info.shape, 1)
    grad_row = jnp.sum(jnp.where(r == c, grad, 0.0), axis=0, keepdims=True)
    rest = states - LANES
    out_ref[...] = jnp.zeros_like(out_ref)
    out_ref[0:states, :] = info[:, 0:LANES]
    out_ref[states : states + 1, :] = grad_row[:, 0:LANES]
    out_ref[LANES + 16 : LANES + 16 + rest, 0:rest] = info[LANES:states, LANES:states]
    out_ref[LANES + 16 + rest : LANES + 17 + rest, 0:rest] = grad_row[:, LANES:states]


def solve_kernel(states, a_ref, b_ref, c_ref, d_ref, info_ref, grad_ref, inc_ref, left, right, x_ref, r_ref, p_ref, gj):
    rest = states - LANES
    rows = LANES + 16
    total = (a_ref[...] + c_ref[...]) + (b_ref[...] + d_ref[...])
    r, c = diagonal(16)
    low = jnp.where(r < rest, total[LANES:rows, :], 0.0)
    corner = jnp.where((r < rest) & (c < rest), total[rows : rows + 16, :], 0.0)
    g0 = total[states : states + 1, :]
    g1 = total[rows + rest : rows + rest + 1, :]
    upper = jnp.concatenate([low, jnp.zeros((LANES - 16, LANES), jnp.float32)], axis=0).T
    info_ref[:, 0, 0:LANES] = jnp.concatenate([total[0:LANES], low[0:rest]], axis=0)
    info_ref[:, 0, LANES:states] = jnp.concatenate([upper[:, 0:rest], corner[0:rest, 0:rest]], axis=0)
    grad_ref[:, 0:LANES] = g0
    grad_ref[:, LANES:states] = g1[:, 0:rest]
    ra, ca = diagonal(LANES)
    eye = (ra == ca).astype(jnp.float32)
    eye_low = (r == c).astype(jnp.float32)
    left[0:LANES, :] = total[0:LANES] + eye
    left[LANES:rows, :] = low
    right[0:LANES, :] = upper
    right[LANES:rows, :] = corner + eye_low

    def to_rows(v):
        return (
            jnp.sum(v[0:LANES] * eye, axis=0, keepdims=True),
            jnp.sum(v[LANES:rows] * eye_low, axis=0, keepdims=True),
        )

    def times(v):
        v0, v1 = to_rows(v)
        return jnp.broadcast_to(jnp.sum(left[...] * v0 + right[...] * v1, axis=1, keepdims=True), (rows, LANES))

    def dot(u, v):
        return jnp.sum(u * v, axis=0, keepdims=True)

    def ratio(num, den):
        return jnp.where(den > 0.0, num / jnp.where(den > 0.0, den, 1.0), 0.0)

    def steps(n, x, res, p, rr):
        for _ in range(n):
            q = times(p)
            alpha = ratio(rr, dot(p, q))
            x = x + alpha * p
            res = res - alpha * q
            new = dot(res, res)
            p = res + ratio(new, rr) * p
            rr = new
        return x, res, p, rr

    col = jnp.concatenate(
        [
            jnp.broadcast_to(jnp.sum(eye * g0, axis=1, keepdims=True), (LANES, LANES)),
            jnp.broadcast_to(jnp.sum(jnp.where(c < rest, eye_low * g1, 0.0), axis=1, keepdims=True), (16, LANES)),
        ],
        axis=0,
    )

    def put(x):
        x0, x1 = to_rows(x)
        inc_ref[:, 0:LANES] = x0
        inc_ref[:, LANES:states] = x1[:, 0:rest]

    def open_after(x):
        res = col - times(x)
        bad = jnp.logical_not(dot(res, res) <= (TOL * TOL) * dot(x, x))
        return jnp.max(bad[:, 0:1].astype(jnp.int32))

    x, res, p, rr = steps(FIRST_STEPS, jnp.zeros_like(col), col, col, dot(col, col))
    put(x)
    still = open_after(x)

    @pl.when(still > 0)
    def _():
        x_ref[...] = x
        r_ref[...] = res
        p_ref[...] = p

        def more(state):
            k, _ = state
            res = r_ref[...]
            x, res, p, _ = steps(MORE_STEPS, x_ref[...], res, p_ref[...], dot(res, res))
            x_ref[...] = x
            r_ref[...] = res
            p_ref[...] = p
            return k + 1, open_after(x)

        _, open_still = lax.while_loop(
            lambda s: (s[0] < MORE_ROUNDS) & (s[1] > 0), more, (jnp.int32(0), jnp.int32(1))
        )
        put(x_ref[...])

        @pl.when(open_still > 0)
        def _():
            wide_r = lax.broadcasted_iota(jnp.int32, (rows, 3 * LANES), 0)
            wide_c = lax.broadcasted_iota(jnp.int32, (rows, 3 * LANES), 1)
            gj[:, 0:LANES] = left[...]
            gj[:, LANES : 2 * LANES] = right[...]
            gj[:, 2 * LANES : 3 * LANES] = col

            def eliminate(i, _):
                a = gj[...]
                row = jnp.sum(jnp.where(wide_r == i, a, 0.0), axis=0, keepdims=True)
                lane = lax.broadcasted_iota(jnp.int32, row.shape, 1)
                pivot = jnp.sum(jnp.where(lane == i, row, 0.0), axis=1, keepdims=True)
                row = row / pivot
                column = jnp.sum(jnp.where(wide_c == i, a, 0.0), axis=1, keepdims=True)
                gj[...] = jnp.where(wide_r == i, row, a - column * row)
                return 0

            lax.fori_loop(0, states, eliminate, 0)
            put(gj[:, 2 * LANES : 3 * LANES])


def shards(state_anom, radiance_anom, inv_noise, innovation, valid_count):
    profiles, local_members, states = state_anom.shape
    slab_width = radiance_anom.shape[2]
    mem = lax.axis_size("mem")
    chan = lax.axis_size("chan")
    members_all = local_members * mem
    f32 = jnp.float32
    both = jnp.concatenate([radiance_anom, state_anom], axis=2)
    own = lax.all_to_all(both, "mem", split_axis=0, concat_axis=1, tiled=True)
    prof = lax.axis_index("mem")
    own_count = lax.dynamic_slice_in_dim(valid_count, prof, 1, 0)
    slots = lax.axis_index("chan") * slab_width + jnp.arange(slab_width, dtype=jnp.int32)
    weight = jnp.where(slots[None, :] < own_count[:, None], inv_noise[None, :], 0.0)
    innov = lax.dynamic_slice_in_dim(innovation, prof, 1, 0)
    rows = LANES + 32
    part = pl.pallas_call(
        functools.partial(slab_kernel, states, members_all),
        out_shape=jax.ShapeDtypeStruct((rows, LANES), f32),
        in_specs=[pl.BlockSpec(memory_space=pltpu.VMEM)] * 3,
        out_specs=pl.BlockSpec(memory_space=pltpu.VMEM),
        name="slab",
    )(own[0], weight, innov)
    parts = [part] + [
        lax.ppermute(part, "chan", [(j, (j + k) % chan) for j in range(chan)]) for k in range(1, chan)
    ]
    square = pltpu.VMEM((LANES + 16, LANES), f32)
    info, grad, inc = pl.pallas_call(
        functools.partial(solve_kernel, states),
        out_shape=[
            jax.ShapeDtypeStruct((states, 1, states), f32),
            jax.ShapeDtypeStruct((1, states), f32),
            jax.ShapeDtypeStruct((1, states), f32),
        ],
        in_specs=[pl.BlockSpec(memory_space=pltpu.VMEM)] * 4,
        out_specs=[pl.BlockSpec(memory_space=pltpu.VMEM)] * 3,
        scratch_shapes=[square] * 5 + [pltpu.VMEM((LANES + 16, 3 * LANES), f32)],
        name="solve",
    )(*parts)
    return (jnp.transpose(info, (1, 0, 2)), grad, inc)


def solution(mesh):
    in_specs = (P(None, "mem", None), P(None, "mem", "chan"), P("chan"), P(None, "chan"), P())
    out_specs = (P("mem", None, None), P("mem", None), P("mem", None))
    return jax.shard_map(shards, mesh=mesh, in_specs=in_specs, out_specs=out_specs, check_vma=False)
```

time: 141 us -> 96.7 us (0.69)
  other arithmetic: 48.7 us -> 4.07 us
  Pallas kernels: 0 us -> 8.68 us
  waiting for transfers between devices: 64.6 us -> 60.3 us
  matrix products: 4.23 us -> 0 us
  between operations: 2.16 us -> 0.68 us
    another operation x13 -> x0, other arithmetic: 43.6 us -> none  [the longest x7 23.8 us: shards(): factor = jnp.linalg.cholesky(system)]
    pallas_call x0 -> x2, Pallas kernels: none -> 8.68 us  [the longest x1 5.31 us: shards(): pl.pallas_call(functools.partial(solve_kernel, states), out_shape=[jax.Sh...]
    all_to_all x2 -> x1, waiting for transfers between devices: 64.6 us -> 56.9 us  [shards(): own = lax.all_to_all(both, 'mem', split_axis=0, concat_axis=1, tiled=True)]
    ppermute x0 -> x3, starting transfers between devices: none -> 4.98 us  [shards(): lax.ppermute(part, 'chan', [(j, (j + k) % chan) for j in range(chan)])]
    all_to_all x2 -> x1, starting transfers between devices: 17.3 us -> 13.1 us  [shards(): own = lax.all_to_all(both, 'mem', split_axis=0, concat_axis=1, tiled=True)]
    ppermute x0 -> x3, waiting for transfers between devices: none -> 3.32 us  [shards(): lax.ppermute(part, 'chan', [(j, (j + k) % chan) for j in range(chan)])]
    dot_general x3 -> x0, matrix products: 2.97 us -> none  [the longest x1 1.28 us: slab_terms(): jnp.einsum('pcs,pct->pst', weighted, cross, precision=lax.Precision.HIGHEST)]
    unnamed x7 -> x14, local copies, waits for them, and re-layouts: 0.82 us -> 2.73 us
  transfers between devices with their start and end apart: 2 -> 4, of which waited for: 2 -> 3; matrix products, arithmetic and copies ran while one was open for 1% -> 3% of each run, Pallas kernels for 0% -> 0%
where the time goes in v1:
time: 96.7 us; the launch traced here: 96.3 us
  waiting for transfers between devices  60.3 us (62%)
  starting transfers between devices  18.1 us (19%)
  Pallas kernels  8.68 us (9%)
  local copies, waits for them, and re-layouts  4.53 us (5%)
  other arithmetic  4.07 us (4%)
    all_to_all x1, waiting for transfers between devices, shards(): own = lax.all_to_all(both, 'mem', split_axis=0, concat_axis=1, tiled=True)  56.9 us
    all_to_all x1, starting transfers between devices, shards(): own = lax.all_to_all(both, 'mem', split_axis=0, concat_axis=1, tiled=True)  13.1 us
    pallas_call x1, Pallas kernels, shards(): pl.pallas_call(functools.partial(solve_kernel, states), out_shape=[jax.Sh...  5.31 us
    ppermute x3, starting transfers between devices, shards(): lax.ppermute(part, 'chan', [(j, (j + k) % chan) for j in range(chan)])  4.98 us
    concatenate x1, other arithmetic, shards(): both = jnp.concatenate([radiance_anom, state_anom], axis=2)  3.42 us
    pallas_call x1, Pallas kernels, shards(): pl.pallas_call(functools.partial(slab_kernel, states, members_all), out_s...  3.38 us
    ppermute x3, waiting for transfers between devices, shards(): lax.ppermute(part, 'chan', [(j, (j + k) % chan) for j in range(chan)])  3.32 us
    unnamed x14, local copies, waits for them, and re-layouts  2.73 us
  transfers between devices with their start and end apart: 4, of which 3 were waited for; matrix products, arithmetic and copies ran while one was open for 3% of the time, Pallas kernels for 0%

profile of v1, /device:TPU:1, one launch (start us, length us, event | category | flops | bytes accessed | tf_op | source)
XLA Modules:
  0.0 96.3 jit_solution(6778783732666250290)
XLA Ops:
  0.6 0.0 copy-start
  0.6 3.4 %pad_maximum_fusion = bf16[64,8,2313]{2,1,0:T(8,128)(2,1)} fusion(bf16[64,8,137]{2,1,0:T(8,128)(2,1)} %param.5, bf16[64,8,2176]{2,1,0:T(8,128)(2,1)} %param.6), kind=kLoop, calls=%fused_computation | loop fusion | flops 4737024 | bytes 4737024 | tf_op jit(solution)/shard_map/concatenate | solution.py:168
  4.1 0.0 copy-start.6
  4.1 0.0 copy-start.5
  4.1 13.1 %all-to-all-start = ((bf16[64,8,2313]{2,1,0:T(8,128)(2,1)}), bf16[64,8,2313]{2,1,0:T(8,128)(2,1)S(1)}, u32[]{:S(2)}, u32[]{:S(2)}) async-start(bf16[64,8,2313]{2,1,0:T(8,128)(2,1)} %pad_maximum_fusion), calls=%async_computation | async-start | bytes 4980736 | tf_op jit(solution)/shard_map/all_to_all | solution.py:169
  17.2 0.0 copy-done.6
  17.2 0.6 dynamic_slice.6
  17.8 0.0 copy-done.5
  17.8 0.6 fusion
  18.4 0.6 select_n.12.weight_ref
  19.1 0.0 copy-done
  19.1 0.6 constant_dynamic-slice_fusion.innov_ref
  19.7 56.9 %all-to-all-done = bf16[64,8,2313]{2,1,0:T(8,128)(2,1)S(1)} async-done(((bf16[64,8,2313]{2,1,0:T(8,128)(2,1)}), bf16[64,8,2313]{2,1,0:T(8,128)(2,1)S(1)}, u32[]{:S(2)}, u32[]{:S(2)}) %all-to-all-start) | async-done | bytes 2368544 | tf_op jit(solution)/shard_map/all_to_all | solution.py:169
  76.6 0.0 copy-start.1
  76.6 1.5 %copy-done.1 = bf16[64,8,2313]{2,1,0:T(8,128)(2,1)} copy-done((bf16[64,8,2313]{2,1,0:T(8,128)(2,1)}, bf16[64,8,2313]{2,1,0:T(8,128)(2,1)S(1)}, u32[]{:S(2)}) %copy-start.1) | copy-done | bytes 2368536
  78.1 3.4 %slab.1.a_ref = f32[160,128]{1,0:T(8,128)} custom-call(bf16[512,2313]{1,0:T(8,128)(2,1)} %bitcast.3, f32[1,2176]{1,0:T(1,128)} %select_n.12.weight_ref, f32[1,2176]{1,0:T(1,128)} %constant_dynamic-slice_fusion.innov_ref), custom_call_target="tpu_custom_call" | custom-call | tf_op jit(solution)/shard_map/slab/pallas_call | solution.py:176
  81.4 1.3 %collective-permute-start = (f32[160,128]{1,0:T(8,128)}, f32[160,128]{1,0:T(8,128)S(1)}, u32[]{:S(2)}, u32[]{:S(2)}) collective-permute-start(f32[160,128]{1,0:T(8,128)} %slab.1.a_ref), channel_id=1, source_target_pairs={{0,1},{1,2},{2,3},{3,0},{4,5},{5,6},{6,7},{7,4},{8,9},{9,10},{10,1... | collective-permute-start | bytes 245768 | tf_op jit(solution)/shard_map/ppermute | solution.py:184
  82.7 2.6 %collective-permute-start.1 = (f32[160,128]{1,0:T(8,128)}, f32[160,128]{1,0:T(8,128)S(1)}, u32[]{:S(2)}, u32[]{:S(2)}) collective-permute-start(f32[160,128]{1,0:T(8,128)} %slab.1.a_ref), channel_id=1, source_target_pairs={{0,2},{1,3},{2,0},{3,1},{4,6},{5,7},{6,4},{7,5},{8,10},{9,11},{10,... | collective-permute-start | bytes 245768 | tf_op jit(solution)/shard_map/ppermute | solution.py:184
  85.4 1.1 %collective-permute-start.2 = (f32[160,128]{1,0:T(8,128)}, f32[160,128]{1,0:T(8,128)S(1)}, u32[]{:S(2)}, u32[]{:S(2)}) collective-permute-start(f32[160,128]{1,0:T(8,128)} %slab.1.a_ref), channel_id=1, source_target_pairs={{0,3},{1,0},{2,1},{3,2},{4,7},{5,4},{6,5},{7,6},{8,11},{9,8},{10,9... | collective-permute-start | bytes 245768 | tf_op jit(solution)/shard_map/ppermute | solution.py:184
  86.4 0.4 collective-permute-done.b_ref
  86.9 0.0 copy-start.2
  86.9 2.9 %collective-permute-done.1.c_ref = f32[160,128]{1,0:T(8,128)S(1)} collective-permute-done((f32[160,128]{1,0:T(8,128)}, f32[160,128]{1,0:T(8,128)S(1)}, u32[]{:S(2)}, u32[]{:S(2)}) %collective-permute-start.1) | collective-permute-done | bytes 81952 | tf_op jit(solution)/shard_map/ppermute | solution.py:184
  89.8 0.0 copy-start.3
  89.8 0.0 collective-permute-done.2.d_ref
  89.8 0.0 copy-done.2
  89.8 0.6 copy-done.3
  90.4 0.0 copy-start.4
  90.4 0.6 copy-done.4
  91.0 5.3 %solve.1 = (f32[137,1,137]{2,1,0:T(1,128)}, f32[1,137]{1,0:T(1,128)}, f32[1,137]{1,0:T(1,128)}) custom-call(f32[160,128]{1,0:T(8,128)} %slab.1.a_ref, f32[160,128]{1,0:T(8,128)} %copy-done.2, f32[160,128]{1,0:T(8,128)} %copy-done.3, f32[160,128]{1,0:T(8,128)} %copy-done.4), custom_call_target="tpu_custom_call" | custom-call | tf_op jit(solution)/shard_map/solve/pallas_call | solution.py:187
Async XLA Ops:
  0.6 18.4 %copy-start = (f32[64,2176]{1,0:T(8,128)S(1)}, f32[64,2176]{1,0:T(8,128)}, u32[]{:S(2)}) copy-start(f32[64,2176]{1,0:T(8,128)} %param.8) | copy-start | bytes 1671172
  4.1 13.1 %copy-start.6 = (s32[64]{0:T(128)S(1)}, s32[64]{0:T(128)}, u32[]{:S(2)}) copy-start(s32[64]{0:T(128)} %param.9) | copy-start | bytes 772
  4.1 13.7 %copy-start.5 = (f32[2176]{0:T(1024)S(1)}, f32[2176]{0:T(1024)}, u32[]{:S(2)}) copy-start(f32[2176]{0:T(1024)} %param.7) | copy-start | bytes 26116
  4.1 72.5 %all-to-all-start = ((bf16[64,8,2313]{2,1,0:T(8,128)(2,1)}), bf16[64,8,2313]{2,1,0:T(8,128)(2,1)S(1)}, u32[]{:S(2)}, u32[]{:S(2)}) async-start(bf16[64,8,2313]{2,1,0:T(8,128)(2,1)} %pad_maximum_fusion), calls=%async_computation | async-start | bytes 4980736 | tf_op jit(solution)/shard_map/all_to_all | solution.py:169
  76.6 1.5 %copy-start.1 = (bf16[64,8,2313]{2,1,0:T(8,128)(2,1)}, bf16[64,8,2313]{2,1,0:T(8,128)(2,1)S(1)}, u32[]{:S(2)}) copy-start(bf16[64,8,2313]{2,1,0:T(8,128)(2,1)S(1)} %all-to-all-done) | copy-start | bytes 7105540
  81.4 5.4 %collective-permute-start = (f32[160,128]{1,0:T(8,128)}, f32[160,128]{1,0:T(8,128)S(1)}, u32[]{:S(2)}, u32[]{:S(2)}) collective-permute-start(f32[160,128]{1,0:T(8,128)} %slab.1.a_ref), channel_id=1, source_target_pairs={{0,1},{1,2},{2,3},{3,0},{4,5},{5,6},{6,7},{7,4},{8,9},{9,10},{10,1... | collective-permute-start | bytes 245768 | tf_op jit(solution)/shard_map/ppermute | solution.py:184
  82.7 7.0 %collective-permute-start.1 = (f32[160,128]{1,0:T(8,128)}, f32[160,128]{1,0:T(8,128)S(1)}, u32[]{:S(2)}, u32[]{:S(2)}) collective-permute-start(f32[160,128]{1,0:T(8,128)} %slab.1.a_ref), channel_id=1, source_target_pairs={{0,2},{1,3},{2,0},{3,1},{4,6},{5,7},{6,4},{7,5},{8,10},{9,11},{10,... | collective-permute-start | bytes 245768 | tf_op jit(solution)/shard_map/ppermute | solution.py:184
  85.4 4.4 %collective-permute-start.2 = (f32[160,128]{1,0:T(8,128)}, f32[160,128]{1,0:T(8,128)S(1)}, u32[]{:S(2)}, u32[]{:S(2)}) collective-permute-start(f32[160,128]{1,0:T(8,128)} %slab.1.a_ref), channel_id=1, source_target_pairs={{0,3},{1,0},{2,1},{3,2},{4,7},{5,4},{6,5},{7,6},{8,11},{9,8},{10,9... | collective-permute-start | bytes 245768 | tf_op jit(solution)/shard_map/ppermute | solution.py:184
  86.9 2.9 %copy-start.2 = (f32[160,128]{1,0:T(8,128)}, f32[160,128]{1,0:T(8,128)S(1)}, u32[]{:S(2)}) copy-start(f32[160,128]{1,0:T(8,128)S(1)} %collective-permute-done.b_ref) | copy-start | bytes 245764
  89.8 0.6 copy-start.3
  90.4 0.6 copy-start.4

commit v2 on v1

--- a/solution.py
+++ b/solution.py
@@ -18,6 +18,31 @@
     r = lax.broadcasted_iota(jnp.int32, (rows, LANES), 0)
     c = lax.broadcasted_iota(jnp.int32, (rows, LANES), 1)
     return r, c
+
+
+PIECES = 8
+
+
+def join_kernel(rad_ref, st_ref, out_ref, held, st, arrived, left):
+    width = rad_ref.shape[2]
+    states = st_ref.shape[2]
+    step = rad_ref.shape[0] // PIECES
+    first = pltpu.make_async_copy(st_ref, st, arrived.at[PIECES])
+    first.start()
+    into, away = [], []
+    for k in range(PIECES):
+        part = pl.ds(k * step, step)
+        into.append(pltpu.make_async_copy(rad_ref.at[part], held.at[part, :, pl.ds(0, width)], arrived.at[k]))
+        away.append(pltpu.make_async_copy(held.at[part], out_ref.at[part], left.at[k]))
+    for copy in into:
+        copy.start()
+    first.wait()
+    held[:, :, width : width + states] = st[...]
+    for come, go in zip(into, away):
+        come.wait()
+        go.start()
+    for copy in away:
+        copy.wait()
 
 
 def slab_kernel(states, members_all, x_ref, weight_ref, innov_ref, out_ref):
@@ -165,7 +190,19 @@
     chan = lax.axis_size("chan")
     members_all = local_members * mem
     f32 = jnp.float32
-    both = jnp.concatenate([radiance_anom, state_anom], axis=2)
+    both = pl.pallas_call(
+        join_kernel,
+        out_shape=jax.ShapeDtypeStruct((profiles, local_members, slab_width + 2 * LANES), jnp.bfloat16),
+        in_specs=[pl.BlockSpec(memory_space=pltpu.HBM)] * 2,
+        out_specs=pl.BlockSpec(memory_space=pltpu.HBM),
+        scratch_shapes=[
+            pltpu.VMEM((profiles, local_members, slab_width + 2 * LANES), jnp.bfloat16),
+            pltpu.VMEM((profiles, local_members, states), jnp.bfloat16),
+            pltpu.SemaphoreType.DMA((PIECES + 1,)),
+            pltpu.SemaphoreType.DMA((PIECES,)),
+        ],
+        name="join",
+    )(radiance_anom, state_anom)
     own = lax.all_to_all(both, "mem", split_axis=0, concat_axis=1, tiled=True)
     prof = lax.axis_index("mem")
     own_count = lax.dynamic_slice_in_dim(valid_count, prof, 1, 0)
@@ -178,6 +215,7 @@
         out_shape=jax.ShapeDtypeStruct((rows, LANES), f32),
         in_specs=[pl.BlockSpec(memory_space=pltpu.VMEM)] * 3,
         out_specs=pl.BlockSpec(memory_space=pltpu.VMEM),
+        compiler_params=pltpu.CompilerParams(vmem_limit_bytes=24 * 2**20),
         name="slab",
     )(own[0], weight, innov)
     parts = [part] + [
@@ -194,6 +232,7 @@
         in_specs=[pl.BlockSpec(memory_space=pltpu.VMEM)] * 4,
         out_specs=[pl.BlockSpec(memory_space=pltpu.VMEM)] * 3,
         scratch_shapes=[square] * 5 + [pltpu.VMEM((LANES + 16, 3 * LANES), f32)],
+        compiler_params=pltpu.CompilerParams(vmem_limit_bytes=8 * 2**20),
         name="solve",
     )(*parts)
     return (jnp.transpose(info, (1, 0, 2)), grad, inc)

time: 96.7 us -> 89.6 us (0.927)
  local copies, waits for them, and re-layouts: 4.53 us -> 0.63 us
  other arithmetic: 4.07 us -> 0.65 us
    concatenate x1 -> x0, other arithmetic: 3.42 us -> none  [shards(): both = jnp.concatenate([radiance_anom, state_anom], axis=2)]
    pallas_call x0 -> x1, Pallas kernels: none -> 2.72 us  [shards(): pl.pallas_call(join_kernel, out_shape=jax.ShapeDtypeStruct((profiles, loc...]
    unnamed x14 -> x6, local copies, waits for them, and re-layouts: 2.73 us -> 0.02 us
    pallas_call x1, Pallas kernels: 3.38 us -> 1.03 us  [shards(): pl.pallas_call(functools.partial(slab_kernel, states, members_all), out_s...]
    all_to_all x1, waiting for transfers between devices: 56.9 us -> 58.1 us  [shards(): own = lax.all_to_all(both, 'mem', split_axis=0, concat_axis=1, tiled=True)]
    pallas_call x1, Pallas kernels: 5.31 us -> 4.31 us  [shards(): pl.pallas_call(functools.partial(solve_kernel, states), out_shape=[jax.Sh...]
  transfers between devices with their start and end apart: 4 -> 4, of which waited for: 3 -> 3; matrix products, arithmetic and copies ran while one was open for 3% -> 1% of each run, Pallas kernels for 0% -> 0%
where the time goes in v2:
time: 89.6 us; the launch traced here: 89.3 us
  waiting for transfers between devices  61.2 us (68%)
  starting transfers between devices  18 us (20%)
  Pallas kernels  8.06 us (9%)
    all_to_all x1, waiting for transfers between devices, shards(): own = lax.all_to_all(both, 'mem', split_axis=0, concat_axis=1, tiled=True)  58.1 us
    all_to_all x1, starting transfers between devices, shards(): own = lax.all_to_all(both, 'mem', split_axis=0, concat_axis=1, tiled=True)  13 us
    ppermute x3, starting transfers between devices, shards(): lax.ppermute(part, 'chan', [(j, (j + k) % chan) for j in range(chan)])  5.06 us
    pallas_call x1, Pallas kernels, shards(): pl.pallas_call(functools.partial(solve_kernel, states), out_shape=[jax.Sh...  4.31 us
    ppermute x3, waiting for transfers between devices, shards(): lax.ppermute(part, 'chan', [(j, (j + k) % chan) for j in range(chan)])  3.11 us
    pallas_call x1, Pallas kernels, shards(): pl.pallas_call(join_kernel, out_shape=jax.ShapeDtypeStruct((profiles, loc...  2.72 us
  transfers between devices with their start and end apart: 4, of which 3 were waited for; matrix products, arithmetic and copies ran while one was open for 1% of the time, Pallas kernels for 0%

profile of v2, /device:TPU:1, one launch (start us, length us, event | category | flops | bytes accessed | tf_op | source)
XLA Modules:
  0.0 89.3 jit_solution(2446664369890031117)
XLA Ops:
  0.6 0.0 copy-start
  0.6 2.7 %join.1 = bf16[64,8,2432]{2,1,0:T(8,128)(2,1)} custom-call(bf16[64,8,2176]{2,1,0:T(8,128)(2,1)} %rad_ref.1, bf16[64,8,137]{2,1,0:T(8,128)(2,1)} %st_ref.1), custom_call_target="tpu_custom_call" | custom-call | tf_op jit(solution)/shard_map/join/pallas_call | solution.py:193
  3.4 0.0 copy-start.2
  3.4 0.0 copy-start.1
  3.4 13.0 %all-to-all-start = ((bf16[64,8,2432]{2,1,0:T(8,128)(2,1)}), bf16[64,8,2432]{2,1,0:T(8,128)(2,1)S(1)}, u32[]{:S(2)}, u32[]{:S(2)}) async-start(bf16[64,8,2432]{2,1,0:T(8,128)(2,1)} %join.1), calls=%async_computation | async-start | bytes 4980736 | tf_op jit(solution)/shard_map/all_to_all | solution.py:206
  16.4 0.0 copy-done.2
  16.4 0.6 dynamic_slice.6
  17.0 0.0 copy-done.1
  17.0 0.6 fusion
  17.7 0.0 copy-done
  17.7 58.1 %all-to-all-done = bf16[64,8,2432]{2,1,0:T(8,128)(2,1)S(1)} async-done(((bf16[64,8,2432]{2,1,0:T(8,128)(2,1)}), bf16[64,8,2432]{2,1,0:T(8,128)(2,1)S(1)}, u32[]{:S(2)}, u32[]{:S(2)}) %all-to-all-start) | async-done | bytes 2490400 | tf_op jit(solution)/shard_map/all_to_all | solution.py:206
  75.8 1.0 %slab.1.a_ref = f32[160,128]{1,0:T(8,128)S(1)} custom-call(bf16[512,2432]{1,0:T(8,128)(2,1)S(1)} %bitcast.3, f32[1,2176]{1,0:T(1,128)S(1)} %select_n.12.weight_ref, f32[1,2176]{1,0:T(1,128)S(1)} %constant_dynamic-slice_fusion.innov_ref), custom_call_target="tpu_custom_call" | custom-call | tf_op jit(solution)/shard_map/slab/pallas_call | solution.py:213
  76.8 1.4 %collective-permute-start = (f32[160,128]{1,0:T(8,128)S(1)}, f32[160,128]{1,0:T(8,128)S(1)}, u32[]{:S(2)}, u32[]{:S(2)}) collective-permute-start(f32[160,128]{1,0:T(8,128)S(1)} %slab.1.a_ref), channel_id=1, source_target_pairs={{0,1},{1,2},{2,3},{3,0},{4,5},{5,6},{6,7},{7,4},{8,9},{9,10},{10,1... | collective-permute-start | bytes 245768 | tf_op jit(solution)/shard_map/ppermute | solution.py:222
  78.2 2.6 %collective-permute-start.1 = (f32[160,128]{1,0:T(8,128)S(1)}, f32[160,128]{1,0:T(8,128)S(1)}, u32[]{:S(2)}, u32[]{:S(2)}) collective-permute-start(f32[160,128]{1,0:T(8,128)S(1)} %slab.1.a_ref), channel_id=1, source_target_pairs={{0,2},{1,3},{2,0},{3,1},{4,6},{5,7},{6,4},{7,5},{8,10},{9,11},{10,... | collective-permute-start | bytes 245768 | tf_op jit(solution)/shard_map/ppermute | solution.py:222
  80.8 1.1 %collective-permute-start.2 = (f32[160,128]{1,0:T(8,128)S(1)}, f32[160,128]{1,0:T(8,128)S(1)}, u32[]{:S(2)}, u32[]{:S(2)}) collective-permute-start(f32[160,128]{1,0:T(8,128)S(1)} %slab.1.a_ref), channel_id=1, source_target_pairs={{0,3},{1,0},{2,1},{3,2},{4,7},{5,4},{6,5},{7,6},{8,11},{9,8},{10,9... | collective-permute-start | bytes 245768 | tf_op jit(solution)/shard_map/ppermute | solution.py:222
  81.9 0.2 collective-permute-done.b_ref
  82.1 2.9 %collective-permute-done.1.c_ref = f32[160,128]{1,0:T(8,128)S(1)} collective-permute-done((f32[160,128]{1,0:T(8,128)S(1)}, f32[160,128]{1,0:T(8,128)S(1)}, u32[]{:S(2)}, u32[]{:S(2)}) %collective-permute-start.1) | collective-permute-done | bytes 81952 | tf_op jit(solution)/shard_map/ppermute | solution.py:222
  85.0 0.0 collective-permute-done.2.d_ref
  85.0 4.3 %solve.1 = (f32[137,1,137]{2,1,0:T(1,128)}, f32[1,137]{1,0:T(1,128)}, f32[1,137]{1,0:T(1,128)}) custom-call(f32[160,128]{1,0:T(8,128)S(1)} %slab.1.a_ref, f32[160,128]{1,0:T(8,128)S(1)} %collective-permute-done.b_ref, f32[160,128]{1,0:T(8,128)S(1)} %collective-permute-done.1.c_ref, f32[160,128]{1,0:T(8,128)S(1)} %collective-permute-done.2.d_ref), custom_call_target="tpu_custom_call" | custom-call | tf_op jit(solution)/shard_map/solve/pallas_call | solution.py:225
  (2 shorter events, 0.0 us)
Async XLA Ops:
  0.6 17.0 %copy-start = (f32[64,2176]{1,0:T(8,128)S(1)}, f32[64,2176]{1,0:T(8,128)}, u32[]{:S(2)}) copy-start(f32[64,2176]{1,0:T(8,128)} %param.8) | copy-start | bytes 1671172
  3.4 13.0 %copy-start.2 = (s32[64]{0:T(128)S(1)}, s32[64]{0:T(128)}, u32[]{:S(2)}) copy-start(s32[64]{0:T(128)} %param.9) | copy-start | bytes 772
  3.4 13.6 %copy-start.1 = (f32[2176]{0:T(1024)S(1)}, f32[2176]{0:T(1024)}, u32[]{:S(2)}) copy-start(f32[2176]{0:T(1024)} %param.7) | copy-start | bytes 26116
  3.4 72.4 %all-to-all-start = ((bf16[64,8,2432]{2,1,0:T(8,128)(2,1)}), bf16[64,8,2432]{2,1,0:T(8,128)(2,1)S(1)}, u32[]{:S(2)}, u32[]{:S(2)}) async-start(bf16[64,8,2432]{2,1,0:T(8,128)(2,1)} %join.1), calls=%async_computation | async-start | bytes 4980736 | tf_op jit(solution)/shard_map/all_to_all | solution.py:206
  76.8 5.3 %collective-permute-start = (f32[160,128]{1,0:T(8,128)S(1)}, f32[160,128]{1,0:T(8,128)S(1)}, u32[]{:S(2)}, u32[]{:S(2)}) collective-permute-start(f32[160,128]{1,0:T(8,128)S(1)} %slab.1.a_ref), channel_id=1, source_target_pairs={{0,1},{1,2},{2,3},{3,0},{4,5},{5,6},{6,7},{7,4},{8,9},{9,10},{10,1... | collective-permute-start | bytes 245768 | tf_op jit(solution)/shard_map/ppermute | solution.py:222
  78.2 6.8 %collective-permute-start.1 = (f32[160,128]{1,0:T(8,128)S(1)}, f32[160,128]{1,0:T(8,128)S(1)}, u32[]{:S(2)}, u32[]{:S(2)}) collective-permute-start(f32[160,128]{1,0:T(8,128)S(1)} %slab.1.a_ref), channel_id=1, source_target_pairs={{0,2},{1,3},{2,0},{3,1},{4,6},{5,7},{6,4},{7,5},{8,10},{9,11},{10,... | collective-permute-start | bytes 245768 | tf_op jit(solution)/shard_map/ppermute | solution.py:222
  80.8 4.2 %collective-permute-start.2 = (f32[160,128]{1,0:T(8,128)S(1)}, f32[160,128]{1,0:T(8,128)S(1)}, u32[]{:S(2)}, u32[]{:S(2)}) collective-permute-start(f32[160,128]{1,0:T(8,128)S(1)} %slab.1.a_ref), channel_id=1, source_target_pairs={{0,3},{1,0},{2,1},{3,2},{4,7},{5,4},{6,5},{7,6},{8,11},{9,8},{10,9... | collective-permute-start | bytes 245768 | tf_op jit(solution)/shard_map/ppermute | solution.py:222

commit v3 on v2

--- a/solution.py
+++ b/solution.py
@@ -10,11 +10,12 @@
 LANES = 128
 TOL = 1e-5
 FIRST_STEPS = 10
-MORE_STEPS = 4
+MORE_STEPS = 6
 MORE_ROUNDS = 8
-
-
-def diagonal(rows):
+PACKED = 96
+
+
+def places(rows):
     r = lax.broadcasted_iota(jnp.int32, (rows, LANES), 0)
     c = lax.broadcasted_iota(jnp.int32, (rows, LANES), 1)
     return r, c
@@ -63,34 +64,53 @@
     c = lax.broadcasted_iota(jnp.int32, info.shape, 1)
     grad_row = jnp.sum(jnp.where(r == c, grad, 0.0), axis=0, keepdims=True)
     rest = states - LANES
-    out_ref[...] = jnp.zeros_like(out_ref)
-    out_ref[0:states, :] = info[:, 0:LANES]
-    out_ref[states : states + 1, :] = grad_row[:, 0:LANES]
-    out_ref[LANES + 16 : LANES + 16 + rest, 0:rest] = info[LANES:states, LANES:states]
-    out_ref[LANES + 16 + rest : LANES + 17 + rest, 0:rest] = grad_row[:, LANES:states]
-
-
-def solve_kernel(states, a_ref, b_ref, c_ref, d_ref, info_ref, grad_ref, inc_ref, left, right, x_ref, r_ref, p_ref, gj):
+    half = LANES // 2
+    other = pltpu.roll(info[half:LANES, 0:LANES], half, 1)
+    r, c = places(half)
+    out_ref[0:half, :] = jnp.where(c < r, other, info[0:half, 0:LANES])
+    out_ref[half:, :] = jnp.zeros((PACKED - half, LANES), jnp.float32)
+    out_ref[half : half + rest, :] = info[LANES:states, 0:LANES]
+    out_ref[half + rest : half + rest + 1, :] = grad_row[:, 0:LANES]
+    out_ref[half + rest + 1 : half + rest + 2, :] = jnp.sum(jnp.where(r == c, other, 0.0), axis=0, keepdims=True)
+    out_ref[half + 16 : half + 16 + rest, 0:rest] = info[LANES:states, LANES:states]
+    out_ref[half + 16 + rest : half + 17 + rest, 0:rest] = grad_row[:, LANES:states]
+
+
+def solve_kernel(
+    states, a_ref, b_ref, c_ref, d_ref, info_ref, grad_ref, inc_ref, info, grad, inc, left, right, x_ref, r_ref, gj, done
+):
     rest = states - LANES
     rows = LANES + 16
-    total = (a_ref[...] + c_ref[...]) + (b_ref[...] + d_ref[...])
-    r, c = diagonal(16)
-    low = jnp.where(r < rest, total[LANES:rows, :], 0.0)
-    corner = jnp.where((r < rest) & (c < rest), total[rows : rows + 16, :], 0.0)
-    g0 = total[states : states + 1, :]
-    g1 = total[rows + rest : rows + rest + 1, :]
+    half = LANES // 2
+    total = (a_ref[...] + b_ref[...]) + (c_ref[...] + d_ref[...])
+    r, c = places(half)
+    ra, ca = places(LANES)
+    last = jnp.where(ca[0:1] < half, total[half + rest + 1 : half + rest + 2, :], 0.0)
+    lower = jnp.where(c < r, total[0:half], 0.0) + jnp.where(c == r, last, 0.0)
+    part = jnp.concatenate([jnp.where(c < r, 0.0, total[0:half]), pltpu.roll(lower, half, 1)], axis=0)
+    square = jnp.where(ra == ca, part, part + part.T)
+    r, c = places(16)
+    low = jnp.where(r < rest, total[half : half + 16, :], 0.0)
+    corner = jnp.where((r < rest) & (c < rest), total[half + 16 : half + 32, :], 0.0)
+    g0 = total[half + rest : half + rest + 1, :]
+    g1 = total[half + 16 + rest : half + 17 + rest, :]
     upper = jnp.concatenate([low, jnp.zeros((LANES - 16, LANES), jnp.float32)], axis=0).T
-    info_ref[:, 0, 0:LANES] = jnp.concatenate([total[0:LANES], low[0:rest]], axis=0)
-    info_ref[:, 0, LANES:states] = jnp.concatenate([upper[:, 0:rest], corner[0:rest, 0:rest]], axis=0)
-    grad_ref[:, 0:LANES] = g0
-    grad_ref[:, LANES:states] = g1[:, 0:rest]
-    ra, ca = diagonal(LANES)
+    info[:, 0, 0:LANES] = jnp.concatenate([square, low[0:rest]], axis=0)
+    info[:, 0, LANES:states] = jnp.concatenate([upper[:, 0:rest], corner[0:rest, 0:rest]], axis=0)
+    grad[:, 0:LANES] = g0
+    grad[:, LANES:states] = g1[:, 0:rest]
     eye = (ra == ca).astype(jnp.float32)
     eye_low = (r == c).astype(jnp.float32)
-    left[0:LANES, :] = total[0:LANES] + eye
+    left[0:LANES, :] = square + eye
     left[LANES:rows, :] = low
     right[0:LANES, :] = upper
     right[LANES:rows, :] = corner + eye_low
+    early = (
+        pltpu.make_async_copy(info, info_ref, done.at[0]),
+        pltpu.make_async_copy(grad, grad_ref, done.at[1]),
+    )
+    for copy in early:
+        copy.start()
 
     def to_rows(v):
         return (
@@ -108,16 +128,23 @@
     def ratio(num, den):
         return jnp.where(den > 0.0, num / jnp.where(den > 0.0, den, 1.0), 0.0)
 
-    def steps(n, x, res, p, rr):
+    def steps(n, x, res, p, s, gamma, alpha):
         for _ in range(n):
-            q = times(p)
-            alpha = ratio(rr, dot(p, q))
+            w = times(res)
+            new = dot(res, res)
+            delta = dot(res, w)
+            if gamma is None:
+                alpha = ratio(new, delta)
+                p, s = res, w
+            else:
+                beta = ratio(new, gamma)
+                alpha = ratio(new, delta - beta * ratio(new, alpha))
+                p = res + beta * p
+                s = w + beta * s
             x = x + alpha * p
-            res = res - alpha * q
-            new = dot(res, res)
-            p = res + ratio(new, rr) * p
-            rr = new
-        return x, res, p, rr
+            res = res - alpha * s
+            gamma = new
+        return x, res
 
     col = jnp.concatenate(
         [
@@ -129,32 +156,30 @@
 
     def put(x):
         x0, x1 = to_rows(x)
-        inc_ref[:, 0:LANES] = x0
-        inc_ref[:, LANES:states] = x1[:, 0:rest]
+        inc[:, 0:LANES] = x0
+        inc[:, LANES:states] = x1[:, 0:rest]
 
     def open_after(x):
         res = col - times(x)
         bad = jnp.logical_not(dot(res, res) <= (TOL * TOL) * dot(x, x))
-        return jnp.max(bad[:, 0:1].astype(jnp.int32))
-
-    x, res, p, rr = steps(FIRST_STEPS, jnp.zeros_like(col), col, col, dot(col, col))
+        return jnp.max(bad[:, 0:1].astype(jnp.int32)), res
+
+    x, _ = steps(FIRST_STEPS, jnp.zeros_like(col), col, None, None, None, None)
     put(x)
-    still = open_after(x)
+    still, res = open_after(x)
 
     @pl.when(still > 0)
     def _():
         x_ref[...] = x
         r_ref[...] = res
-        p_ref[...] = p
 
         def more(state):
             k, _ = state
-            res = r_ref[...]
-            x, res, p, _ = steps(MORE_STEPS, x_ref[...], res, p_ref[...], dot(res, res))
+            x, _ = steps(MORE_STEPS, x_ref[...], r_ref[...], None, None, None, None)
+            still, res = open_after(x)
             x_ref[...] = x
             r_ref[...] = res
-            p_ref[...] = p
-            return k + 1, open_after(x)
+            return k + 1, still
 
         _, open_still = lax.while_loop(
             lambda s: (s[0] < MORE_ROUNDS) & (s[1] > 0), more, (jnp.int32(0), jnp.int32(1))
@@ -181,6 +206,12 @@
 
             lax.fori_loop(0, states, eliminate, 0)
             put(gj[:, 2 * LANES : 3 * LANES])
+
+    late = pltpu.make_async_copy(inc, inc_ref, done.at[2])
+    late.start()
+    for copy in early:
+        copy.wait()
+    late.wait()
 
 
 def shards(state_anom, radiance_anom, inv_noise, innovation, valid_count):
@@ -209,29 +240,27 @@
     slots = lax.axis_index("chan") * slab_width + jnp.arange(slab_width, dtype=jnp.int32)
     weight = jnp.where(slots[None, :] < own_count[:, None], inv_noise[None, :], 0.0)
     innov = lax.dynamic_slice_in_dim(innovation, prof, 1, 0)
-    rows = LANES + 32
     part = pl.pallas_call(
         functools.partial(slab_kernel, states, members_all),
-        out_shape=jax.ShapeDtypeStruct((rows, LANES), f32),
+        out_shape=jax.ShapeDtypeStruct((PACKED, LANES), f32),
         in_specs=[pl.BlockSpec(memory_space=pltpu.VMEM)] * 3,
         out_specs=pl.BlockSpec(memory_space=pltpu.VMEM),
         compiler_params=pltpu.CompilerParams(vmem_limit_bytes=24 * 2**20),
         name="slab",
     )(own[0], weight, innov)
     parts = [part] + [
-        lax.ppermute(part, "chan", [(j, (j + k) % chan) for j in range(chan)]) for k in range(1, chan)
+        lax.ppermute(part, "chan", [(j, (j + k) % chan) for j in range(chan)]) for k in (2, 1, 3)
     ]
+    outs = [(states, 1, states), (1, states), (1, states)]
     square = pltpu.VMEM((LANES + 16, LANES), f32)
     info, grad, inc = pl.pallas_call(
         functools.partial(solve_kernel, states),
-        out_shape=[
-            jax.ShapeDtypeStruct((states, 1, states), f32),
-            jax.ShapeDtypeStruct((1, states), f32),
-            jax.ShapeDtypeStruct((1, states), f32),
-        ],
+        out_shape=[jax.ShapeDtypeStruct(shape, f32) for shape in outs],
         in_specs=[pl.BlockSpec(memory_space=pltpu.VMEM)] * 4,
-        out_specs=[pl.BlockSpec(memory_space=pltpu.VMEM)] * 3,
-        scratch_shapes=[square] * 5 + [pltpu.VMEM((LANES + 16, 3 * LANES), f32)],
+        out_specs=[pl.BlockSpec(memory_space=pltpu.HBM)] * 3,
+        scratch_shapes=[pltpu.VMEM(shape, f32) for shape in outs]
+        + [square] * 4
+        + [pltpu.VMEM((LANES + 16, 3 * LANES), f32), pltpu.SemaphoreType.DMA((3,))],
         compiler_params=pltpu.CompilerParams(vmem_limit_bytes=8 * 2**20),
         name="solve",
     )(*parts)

time: 89.6 us -> 89.5 us (level)
  waiting for transfers between devices: 61.2 us -> 59.6 us
    ppermute x3, waiting for transfers between devices: 3.11 us -> 1.48 us  [shards(): lax.ppermute(part, 'chan', [(j, (j + k) % chan) for j in range(chan)])]
  transfers between devices with their start and end apart: 4 -> 4, of which waited for: 3 -> 2; matrix products, arithmetic and copies ran while one was open for 1% -> 1% of each run, Pallas kernels for 0% -> 0%
where the time goes in v3:
time: 89.5 us; the launch traced here: 88.6 us
  waiting for transfers between devices  59.6 us (67%)
  starting transfers between devices  18.7 us (21%)
  Pallas kernels  8.32 us (9%)
    all_to_all x1, waiting for transfers between devices, shards(): own = lax.all_to_all(both, 'mem', split_axis=0, concat_axis=1, tiled=True)  58.1 us
    all_to_all x1, starting transfers between devices, shards(): own = lax.all_to_all(both, 'mem', split_axis=0, concat_axis=1, tiled=True)  13 us
    ppermute x3, starting transfers between devices, shards(): lax.ppermute(part, 'chan', [(j, (j + k) % chan) for j in range(chan)])  5.67 us
    pallas_call x1, Pallas kernels, shards(): pl.pallas_call(functools.partial(solve_kernel, states), out_shape=[jax.Sh...  4.54 us
    pallas_call x1, Pallas kernels, shards(): pl.pallas_call(join_kernel, out_shape=jax.ShapeDtypeStruct((profiles, loc...  2.72 us
  transfers between devices with their start and end apart: 4, of which 2 were waited for; matrix products, arithmetic and copies ran while one was open for 1% of the time, Pallas kernels for 0%

profile of v3, /device:TPU:1, one launch (start us, length us, event | category | flops | bytes accessed | tf_op | source)
XLA Modules:
  0.0 88.6 jit_solution(17192577896713696439)
XLA Ops:
  0.6 0.0 copy-start
  0.6 2.7 %join.1 = bf16[64,8,2432]{2,1,0:T(8,128)(2,1)} custom-call(bf16[64,8,2176]{2,1,0:T(8,128)(2,1)} %rad_ref.1, bf16[64,8,137]{2,1,0:T(8,128)(2,1)} %st_ref.1), custom_call_target="tpu_custom_call" | custom-call | tf_op jit(solution)/shard_map/join/pallas_call | solution.py:224
  3.4 0.0 copy-start.2
  3.4 0.0 copy-start.1
  3.4 13.0 %all-to-all-start = ((bf16[64,8,2432]{2,1,0:T(8,128)(2,1)}), bf16[64,8,2432]{2,1,0:T(8,128)(2,1)S(1)}, u32[]{:S(2)}, u32[]{:S(2)}) async-start(bf16[64,8,2432]{2,1,0:T(8,128)(2,1)} %join.1), calls=%async_computation | async-start | bytes 4980736 | tf_op jit(solution)/shard_map/all_to_all | solution.py:237
  16.4 0.0 copy-done.2
  16.4 0.6 dynamic_slice.6
  17.0 0.0 copy-done.1
  17.0 0.6 fusion
  17.7 0.0 copy-done
  17.7 58.1 %all-to-all-done = bf16[64,8,2432]{2,1,0:T(8,128)(2,1)S(1)} async-done(((bf16[64,8,2432]{2,1,0:T(8,128)(2,1)}), bf16[64,8,2432]{2,1,0:T(8,128)(2,1)S(1)}, u32[]{:S(2)}, u32[]{:S(2)}) %all-to-all-start) | async-done | bytes 2490400 | tf_op jit(solution)/shard_map/all_to_all | solution.py:237
  75.8 1.1 %slab.1.a_ref = f32[96,128]{1,0:T(8,128)S(1)} custom-call(bf16[512,2432]{1,0:T(8,128)(2,1)S(1)} %bitcast.3, f32[1,2176]{1,0:T(1,128)S(1)} %select_n.12.weight_ref, f32[1,2176]{1,0:T(1,128)S(1)} %constant_dynamic-slice_fusion.innov_ref), custom_call_target="tpu_custom_call" | custom-call | tf_op jit(solution)/shard_map/slab/pallas_call | solution.py:243
  76.9 3.0 %collective-permute-start = (f32[96,128]{1,0:T(8,128)S(1)}, f32[96,128]{1,0:T(8,128)S(1)}, u32[]{:S(2)}, u32[]{:S(2)}) collective-permute-start(f32[96,128]{1,0:T(8,128)S(1)} %slab.1.a_ref), channel_id=1, source_target_pairs={{0,2},{1,3},{2,0},{3,1},{4,6},{5,7},{6,4},{7,5},{8,10},{9,11},{10,... | collective-permute-start | bytes 147464 | tf_op jit(solution)/shard_map/ppermute | solution.py:252
  79.9 0.4 collective-permute-start.1
  80.3 2.3 %collective-permute-start.2 = (f32[96,128]{1,0:T(8,128)S(1)}, f32[96,128]{1,0:T(8,128)S(1)}, u32[]{:S(2)}, u32[]{:S(2)}) collective-permute-start(f32[96,128]{1,0:T(8,128)S(1)} %slab.1.a_ref), channel_id=1, source_target_pairs={{0,3},{1,0},{2,1},{3,2},{4,7},{5,4},{6,5},{7,6},{8,11},{9,8},{10,9... | collective-permute-start | bytes 147464 | tf_op jit(solution)/shard_map/ppermute | solution.py:252
  82.6 0.0 collective-permute-done.b_ref
  82.6 1.5 %collective-permute-done.1.c_ref = f32[96,128]{1,0:T(8,128)S(1)} collective-permute-done((f32[96,128]{1,0:T(8,128)S(1)}, f32[96,128]{1,0:T(8,128)S(1)}, u32[]{:S(2)}, u32[]{:S(2)}) %collective-permute-start.1) | collective-permute-done | bytes 49184 | tf_op jit(solution)/shard_map/ppermute | solution.py:252
  84.0 0.0 collective-permute-done.2.d_ref
  84.0 4.5 %solve.1 = (f32[137,1,137]{2,1,0:T(1,128)}, f32[1,137]{1,0:T(1,128)}, f32[1,137]{1,0:T(1,128)}) custom-call(f32[96,128]{1,0:T(8,128)S(1)} %slab.1.a_ref, f32[96,128]{1,0:T(8,128)S(1)} %collective-permute-done.b_ref, f32[96,128]{1,0:T(8,128)S(1)} %collective-permute-done.1.c_ref, f32[96,128]{1,0:T(8,128)S(1)} %collective-permute-done.2.d_ref), custom_call_target="tpu_custom_call" | custom-call | tf_op jit(solution)/shard_map/solve/pallas_call | solution.py:256
  (2 shorter events, 0.0 us)
Async XLA Ops:
  0.6 17.0 %copy-start = (f32[64,2176]{1,0:T(8,128)S(1)}, f32[64,2176]{1,0:T(8,128)}, u32[]{:S(2)}) copy-start(f32[64,2176]{1,0:T(8,128)} %param.8) | copy-start | bytes 1671172
  3.4 13.0 %copy-start.2 = (s32[64]{0:T(128)S(1)}, s32[64]{0:T(128)}, u32[]{:S(2)}) copy-start(s32[64]{0:T(128)} %param.9) | copy-start | bytes 772
  3.4 13.6 %copy-start.1 = (f32[2176]{0:T(1024)S(1)}, f32[2176]{0:T(1024)}, u32[]{:S(2)}) copy-start(f32[2176]{0:T(1024)} %param.7) | copy-start | bytes 26116
  3.4 72.4 %all-to-all-start = ((bf16[64,8,2432]{2,1,0:T(8,128)(2,1)}), bf16[64,8,2432]{2,1,0:T(8,128)(2,1)S(1)}, u32[]{:S(2)}, u32[]{:S(2)}) async-start(bf16[64,8,2432]{2,1,0:T(8,128)(2,1)} %join.1), calls=%async_computation | async-start | bytes 4980736 | tf_op jit(solution)/shard_map/all_to_all | solution.py:237
  76.9 5.7 %collective-permute-start = (f32[96,128]{1,0:T(8,128)S(1)}, f32[96,128]{1,0:T(8,128)S(1)}, u32[]{:S(2)}, u32[]{:S(2)}) collective-permute-start(f32[96,128]{1,0:T(8,128)S(1)} %slab.1.a_ref), channel_id=1, source_target_pairs={{0,2},{1,3},{2,0},{3,1},{4,6},{5,7},{6,4},{7,5},{8,10},{9,11},{10,... | collective-permute-start | bytes 147464 | tf_op jit(solution)/shard_map/ppermute | solution.py:252
  79.9 4.2 %collective-permute-start.1 = (f32[96,128]{1,0:T(8,128)S(1)}, f32[96,128]{1,0:T(8,128)S(1)}, u32[]{:S(2)}, u32[]{:S(2)}) collective-permute-start(f32[96,128]{1,0:T(8,128)S(1)} %slab.1.a_ref), channel_id=1, source_target_pairs={{0,1},{1,2},{2,3},{3,0},{4,5},{5,6},{6,7},{7,4},{8,9},{9,10},{10,1... | collective-permute-start | bytes 147464 | tf_op jit(solution)/shard_map/ppermute | solution.py:252
  80.3 3.8 %collective-permute-start.2 = (f32[96,128]{1,0:T(8,128)S(1)}, f32[96,128]{1,0:T(8,128)S(1)}, u32[]{:S(2)}, u32[]{:S(2)}) collective-permute-start(f32[96,128]{1,0:T(8,128)S(1)} %slab.1.a_ref), channel_id=1, source_target_pairs={{0,3},{1,0},{2,1},{3,2},{4,7},{5,4},{6,5},{7,6},{8,11},{9,8},{10,9... | collective-permute-start | bytes 147464 | tf_op jit(solution)/shard_map/ppermute | solution.py:252

commit v4 on v3

--- a/solution.py
+++ b/solution.py
@@ -21,33 +21,123 @@
     return r, c
 
 
-PIECES = 8
-
-
-def join_kernel(rad_ref, st_ref, out_ref, held, st, arrived, left):
+SIZE_X, SIZE_Z, SIZE_C = 4, 8, 2
+ACROSS = tuple((dx, dc) for dx in range(SIZE_X) for dc in range(SIZE_C))
+NEAR = (2, -2, 1, -1, 0)
+FAR = (4, 3, -3)
+SENT = len(NEAR) - 1 + len(ACROSS) - 1
+
+
+def partner(x, z, c):
+    return (x % SIZE_X * SIZE_Z + z % SIZE_Z) * SIZE_C + c % SIZE_C
+
+
+def spread_kernel(rad_ref, st_ref, *refs):
+    outs, own, held, (st, arrived, left) = refs[:SENT], refs[SENT : SENT + 2], refs[SENT + 2 : -3], refs[-3:]
     width = rad_ref.shape[2]
     states = st_ref.shape[2]
-    step = rad_ref.shape[0] // PIECES
-    first = pltpu.make_async_copy(st_ref, st, arrived.at[PIECES])
+    me = lax.axis_index("mem")
+    x, z, c = me // (SIZE_Z * SIZE_C), me // SIZE_C % SIZE_Z, me % SIZE_C
+    first = pltpu.make_async_copy(st_ref, st, arrived.at[SIZE_X * SIZE_Z * SIZE_C])
     first.start()
-    into, away = [], []
-    for k in range(PIECES):
-        part = pl.ds(k * step, step)
-        into.append(pltpu.make_async_copy(rad_ref.at[part], held.at[part, :, pl.ds(0, width)], arrived.at[k]))
-        away.append(pltpu.make_async_copy(held.at[part], out_ref.at[part], left.at[k]))
-    for copy in into:
-        copy.start()
+    near = held[: len(NEAR) - 1] + own[:1]
+    far = own[1:] + held[len(NEAR) - 1 :]
+    groups = [(near[i], [(k, dz, o) for k, o in enumerate(ACROSS)]) for i, dz in enumerate(NEAR)]
+    groups += [(far[i], [(k, dz, o) for k, dz in enumerate(FAR)]) for i, o in enumerate(ACROSS)]
+    groups.sort(key=lambda group: any(group[0] is ref for ref in own))
+    copies, count = [], 0
+    for ref, slots in groups:
+        copies.append([])
+        for k, dz, (dx, dc) in slots:
+            p = lax.rem(x + dx, SIZE_X) * (SIZE_Z * SIZE_C) + lax.rem(z + dz + SIZE_Z, SIZE_Z) * SIZE_C + lax.rem(c + dc, SIZE_C)
+            copy = pltpu.make_async_copy(rad_ref.at[p], ref.at[k, :, pl.ds(0, width)], arrived.at[count])
+            copy.start()
+            copies[-1].append((copy, k, p))
+            count += 1
     first.wait()
-    held[:, :, width : width + states] = st[...]
-    for come, go in zip(into, away):
-        come.wait()
-        go.start()
+    for (ref, _), group in zip(groups, copies):
+        for _, k, p in group:
+            ref[k, :, width : width + states] = st[p]
+    away = []
+    for (ref, _), group in zip(groups, copies):
+        for copy, _, _ in group:
+            copy.wait()
+        for i, source in enumerate(held):
+            if source is ref:
+                away.append(pltpu.make_async_copy(ref, outs[i], left.at[i]))
+                away[-1].start()
     for copy in away:
         copy.wait()
 
 
-def slab_kernel(states, members_all, x_ref, weight_ref, innov_ref, out_ref):
+def swap_kernel(many, *refs):
+    come, go = refs[:many], refs[many:]
+    for i, ref in enumerate(come):
+        for j, out in enumerate(go):
+            out[i] = ref[j]
+
+
+def in_vmem(kernel, outs, count, **more):
+    return pl.pallas_call(
+        kernel,
+        out_shape=outs,
+        in_specs=[pl.BlockSpec(memory_space=pltpu.VMEM)] * count,
+        out_specs=[pl.BlockSpec(memory_space=pltpu.VMEM)] * len(outs),
+        compiler_params=pltpu.CompilerParams(vmem_limit_bytes=20 * 2**20),
+        **more,
+    )
+
+
+def moved(a, dx, dz, dc):
+    pairs = [
+        (partner(x, z, c), partner(x + dx, z + dz, c + dc))
+        for x in range(SIZE_X)
+        for z in range(SIZE_Z)
+        for c in range(SIZE_C)
+    ]
+    return lax.ppermute(a, "mem", pairs)
+
+
+def gathered(rad, st):
+    members, width = rad.shape[1], rad.shape[2] + 2 * LANES
+    tall = [jax.ShapeDtypeStruct((len(ACROSS), members, width), rad.dtype)]
+    flat = [jax.ShapeDtypeStruct((len(FAR), members, width), rad.dtype)]
+    five = [jax.ShapeDtypeStruct((len(NEAR), members, width), rad.dtype)]
+    sent = tall * (len(NEAR) - 1) + flat * (len(ACROSS) - 1)
+    own = tall + flat
+    spread = pl.pallas_call(
+        spread_kernel,
+        out_shape=sent + [pltpu.VMEM(a.shape, a.dtype) for a in own],
+        in_specs=[pl.BlockSpec(memory_space=pltpu.HBM)] * 2,
+        out_specs=[pl.BlockSpec(memory_space=pltpu.HBM)] * SENT + [pl.BlockSpec(memory_space=pltpu.VMEM)] * 2,
+        scratch_shapes=[pltpu.VMEM(a.shape, a.dtype) for a in sent]
+        + [
+            pltpu.VMEM(st.shape, st.dtype),
+            pltpu.SemaphoreType.DMA((st.shape[0] + 1,)),
+            pltpu.SemaphoreType.DMA((SENT,)),
+        ],
+        compiler_params=pltpu.CompilerParams(vmem_limit_bytes=59 * 10**6),
+        name="spread",
+    )(rad, st)
+    near = spread[: len(NEAR) - 1] + spread[SENT : SENT + 1]
+    far = spread[SENT + 1 :] + spread[len(NEAR) - 1 : SENT]
+    near = [a if dz == 0 else moved(a, 0, dz, 0) for a, dz in zip(near, NEAR)]
+    far = [a if o == (0, 0) else moved(a, o[0], 0, o[1]) for a, o in zip(far, ACROSS)]
+    far = in_vmem(functools.partial(swap_kernel, len(ACROSS)), tall * len(FAR), len(ACROSS))(*far)
+    far = [moved(a, 0, dz, 0) for a, dz in zip(far, FAR)]
+    near = in_vmem(functools.partial(swap_kernel, len(NEAR)), five * len(ACROSS), len(NEAR))(*near)
+    near = [a if o == (0, 0) else moved(a, o[0], 0, o[1]) for a, o in zip(near, ACROSS)]
+    return far + near
+
+
+def slab_kernel(states, members_all, *refs):
+    parts, (weight_ref, innov_ref, out_ref, x_ref) = refs[:-4], refs[-4:]
     width = weight_ref.shape[1]
+    at = 0
+    for part in parts:
+        rows = part.shape[0] * part.shape[1]
+        x_ref[at : at + rows, :] = part[...].reshape(rows, part.shape[2])
+        at += rows
     rad = x_ref[:, 0:width]
     st = x_ref[:, width : width + states]
     cross = lax.dot_general(st, rad, (((0,), (0,)), ((), ())), preferred_element_type=jnp.float32)
@@ -215,26 +305,13 @@
 
 
 def shards(state_anom, radiance_anom, inv_noise, innovation, valid_count):
-    profiles, local_members, states = state_anom.shape
+    _, local_members, states = state_anom.shape
     slab_width = radiance_anom.shape[2]
     mem = lax.axis_size("mem")
     chan = lax.axis_size("chan")
     members_all = local_members * mem
     f32 = jnp.float32
-    both = pl.pallas_call(
-        join_kernel,
-        out_shape=jax.ShapeDtypeStruct((profiles, local_members, slab_width + 2 * LANES), jnp.bfloat16),
-        in_specs=[pl.BlockSpec(memory_space=pltpu.HBM)] * 2,
-        out_specs=pl.BlockSpec(memory_space=pltpu.HBM),
-        scratch_shapes=[
-            pltpu.VMEM((profiles, local_members, slab_width + 2 * LANES), jnp.bfloat16),
-            pltpu.VMEM((profiles, local_members, states), jnp.bfloat16),
-            pltpu.SemaphoreType.DMA((PIECES + 1,)),
-            pltpu.SemaphoreType.DMA((PIECES,)),
-        ],
-        name="join",
-    )(radiance_anom, state_anom)
-    own = lax.all_to_all(both, "mem", split_axis=0, concat_axis=1, tiled=True)
+    blocks = gathered(radiance_anom, state_anom)
     prof = lax.axis_index("mem")
     own_count = lax.dynamic_slice_in_dim(valid_count, prof, 1, 0)
     slots = lax.axis_index("chan") * slab_width + jnp.arange(slab_width, dtype=jnp.int32)
@@ -243,11 +320,12 @@
     part = pl.pallas_call(
         functools.partial(slab_kernel, states, members_all),
         out_shape=jax.ShapeDtypeStruct((PACKED, LANES), f32),
-        in_specs=[pl.BlockSpec(memory_space=pltpu.VMEM)] * 3,
+        in_specs=[pl.BlockSpec(memory_space=pltpu.VMEM)] * (len(blocks) + 2),
         out_specs=pl.BlockSpec(memory_space=pltpu.VMEM),
+        scratch_shapes=[pltpu.VMEM((members_all, slab_width + 2 * LANES), jnp.bfloat16)],
         compiler_params=pltpu.CompilerParams(vmem_limit_bytes=24 * 2**20),
         name="slab",
-    )(own[0], weight, innov)
+    )(*blocks, weight, innov)
     parts = [part] + [
         lax.ppermute(part, "chan", [(j, (j + k) % chan) for j in range(chan)]) for k in (2, 1, 3)
     ]

time: 89.5 us -> 108 us (1.21)
  starting transfers between devices: 18.7 us -> 45.6 us
  waiting for transfers between devices: 59.6 us -> 48.9 us
  Pallas kernels: 8.32 us -> 10.7 us
    all_to_all x1 -> x0, waiting for transfers between devices: 58.1 us -> none  [shards(): own = lax.all_to_all(both, 'mem', split_axis=0, concat_axis=1, tiled=True)]
    ppermute x0 -> x21, waiting for transfers between devices: none -> 47 us  [moved(): return lax.ppermute(a, 'mem', pairs)]
    ppermute x0 -> x21, starting transfers between devices: none -> 40 us  [moved(): return lax.ppermute(a, 'mem', pairs)]
    all_to_all x1 -> x0, starting transfers between devices: 13 us -> none  [shards(): own = lax.all_to_all(both, 'mem', split_axis=0, concat_axis=1, tiled=True)]
    pallas_call x1 -> x3, Pallas kernels: 2.72 us -> 4.06 us  [the longest x1 3.03 us: gathered(): pl.pallas_call(spread_kernel, out_shape=sent + [pltpu.VMEM(a.shape, a.dty...]
  transfers between devices with their start and end apart: 4 -> 24, of which waited for: 2 -> 10; matrix products, arithmetic and copies ran while one was open for 1% -> 1% of each run, Pallas kernels for 0% -> 1%
where the time goes in v4:
time: 108 us; the launch traced here: 107 us
  waiting for transfers between devices  48.9 us (45%)
  starting transfers between devices  45.6 us (42%)
  Pallas kernels  10.7 us (10%)
    ppermute x21, waiting for transfers between devices, moved(): return lax.ppermute(a, 'mem', pairs)  47 us
    ppermute x21, starting transfers between devices, moved(): return lax.ppermute(a, 'mem', pairs)  40 us
    ppermute x3, starting transfers between devices, shards(): lax.ppermute(part, 'chan', [(j, (j + k) % chan) for j in range(chan)])  5.59 us
    pallas_call x1, Pallas kernels, shards(): pl.pallas_call(functools.partial(solve_kernel, states), out_shape=[jax.Sh...  5.58 us
    pallas_call x1, Pallas kernels, gathered(): pl.pallas_call(spread_kernel, out_shape=sent + [pltpu.VMEM(a.shape, a.dty...  3.03 us
  transfers between devices with their start and end apart: 24, of which 10 were waited for; matrix products, arithmetic and copies ran while one was open for 1% of the time, Pallas kernels for 1%

profile of v4, /device:TPU:1, one launch (start us, length us, event | category | flops | bytes accessed | tf_op | source)
XLA Modules:
  0.0 107.4 jit_solution(14904250380286671087)
XLA Ops:
  0.7 3.0 %spread.1 = (bf16[8,8,2432]{2,1,0:T(8,128)(2,1)}, bf16[8,8,2432]{2,1,0:T(8,128)(2,1)}, bf16[8,8,2432]{2,1,0:T(8,128)(2,1)}, bf16[8,8,2432]{2,1,0:T(8,128)(2,1)},...) custom-call(bf16[64,8,2176]{2,1,0:T(8,128)(2,1)} %rad_ref.1, ...), custom_call_target="tpu_custom_call" | custom-call | tf_op jit(solution)/shard_map/spread/pallas_call | solution.py:108
  3.7 3.3 %collective-permute-start = (bf16[3,8,2432]{2,1,0:T(8,128)(2,1)}, bf16[3,8,2432]{2,1,0:T(8,128)(2,1)S(1)}, u32[]{:S(2)}, u32[]{:S(2)}) collective-permute-start(bf16[3,8,2432]{2,1,0:T(8,128)(2,1)} %get-tuple-element.31), channel_id=1, source_target_pairs={{0,4},{4,0},{8,12},{12,8},{16,20},{20,16},{24,28},{28,24},{32,36},... | collective-permute-start | bytes 350216 | tf_op jit(solution)/shard_map/ppermute | solution.py:98
  7.0 1.0 collective-permute-start.2
  8.0 3.1 %collective-permute-start.3 = (bf16[3,8,2432]{2,1,0:T(8,128)(2,1)}, bf16[3,8,2432]{2,1,0:T(8,128)(2,1)S(1)}, u32[]{:S(2)}, u32[]{:S(2)}) collective-permute-start(bf16[3,8,2432]{2,1,0:T(8,128)(2,1)} %get-tuple-element.34), channel_id=1, source_target_pairs={{0,128},{4,132},{8,136},{12,140},{16,144},{20,148},{24,152},{28,15... | collective-permute-start | bytes 350216 | tf_op jit(solution)/shard_map/ppermute | solution.py:98
  11.2 3.0 %collective-permute-start.10 = (bf16[8,8,2432]{2,1,0:T(8,128)(2,1)}, bf16[8,8,2432]{2,1,0:T(8,128)(2,1)S(1)}, u32[]{:S(2)}, u32[]{:S(2)}) collective-permute-start(bf16[8,8,2432]{2,1,0:T(8,128)(2,1)} %get-tuple-element.41), channel_id=1, source_target_pairs={{0,16},{4,20},{8,24},{12,28},{16,32},{20,36},{24,40},{28,44},{32,4... | collective-permute-start | bytes 933896 | tf_op jit(solution)/shard_map/ppermute | solution.py:98
  14.2 3.1 %collective-permute-start.11 = (bf16[8,8,2432]{2,1,0:T(8,128)(2,1)}, bf16[8,8,2432]{2,1,0:T(8,128)(2,1)S(1)}, u32[]{:S(2)}, u32[]{:S(2)}) collective-permute-start(bf16[8,8,2432]{2,1,0:T(8,128)(2,1)} %get-tuple-element.42), channel_id=1, source_target_pairs={{0,48},{4,52},{8,56},{12,60},{16,0},{20,4},{24,8},{28,12},{32,16},... | collective-permute-start | bytes 933896 | tf_op jit(solution)/shard_map/ppermute | solution.py:98
  17.4 3.7 %collective-permute-done.2.refs_3_ = bf16[3,8,2432]{2,1,0:T(8,128)(2,1)S(1)} collective-permute-done((bf16[3,8,2432]{2,1,0:T(8,128)(2,1)}, bf16[3,8,2432]{2,1,0:T(8,128)(2,1)S(1)}, u32[]{:S(2)}, u32[]{:S(2)}) %collective-permute-start.2) | collective-permute-done | bytes 116768 | tf_op jit(solution)/shard_map/ppermute | solution.py:98
  21.2 4.8 %collective-permute-start.13 = (bf16[8,8,2432]{2,1,0:T(8,128)(2,1)}, bf16[8,8,2432]{2,1,0:T(8,128)(2,1)S(1)}, u32[]{:S(2)}, u32[]{:S(2)}) collective-permute-start(bf16[8,8,2432]{2,1,0:T(8,128)(2,1)} %get-tuple-element.44), channel_id=1, source_target_pairs={{0,56},{4,60},{8,0},{12,4},{16,8},{20,12},{24,16},{28,20},{32,24},... | collective-permute-start | bytes 933896 | tf_op jit(solution)/shard_map/ppermute | solution.py:98
  26.3 1.8 %collective-permute-start.6 = (bf16[3,8,2432]{2,1,0:T(8,128)(2,1)}, bf16[3,8,2432]{2,1,0:T(8,128)(2,1)S(1)}, u32[]{:S(2)}, u32[]{:S(2)}) collective-permute-start(bf16[3,8,2432]{2,1,0:T(8,128)(2,1)} %get-tuple-element.37), channel_id=1, source_target_pairs={{0,196},{4,192},{8,204},{12,200},{16,212},{20,208},{24,220},{28,21... | collective-permute-start | bytes 350216 | tf_op jit(solution)/shard_map/ppermute | solution.py:98
  28.0 4.2 %collective-permute-done.6.refs_7_ = bf16[3,8,2432]{2,1,0:T(8,128)(2,1)S(1)} collective-permute-done((bf16[3,8,2432]{2,1,0:T(8,128)(2,1)}, bf16[3,8,2432]{2,1,0:T(8,128)(2,1)S(1)}, u32[]{:S(2)}, u32[]{:S(2)}) %collective-permute-start.6) | collective-permute-done | bytes 116768 | tf_op jit(solution)/shard_map/ppermute | solution.py:98
  32.2 0.9 shard_map.76
  33.6 2.5 %collective-permute-start.8 = (bf16[8,8,2432]{2,1,0:T(8,128)(2,1)}, bf16[8,8,2432]{2,1,0:T(8,128)(2,1)S(1)}, u32[]{:S(2)}, u32[]{:S(2)}) collective-permute-start(bf16[8,8,2432]{2,1,0:T(8,128)(2,1)} %get-tuple-element.39), channel_id=1, source_target_pairs={{0,24},{4,28},{8,32},{12,36},{16,40},{20,44},{24,48},{28,52},{32,5... | collective-permute-start | bytes 933896 | tf_op jit(solution)/shard_map/ppermute | solution.py:98
  36.1 2.0 %collective-permute-start.9 = (bf16[8,8,2432]{2,1,0:T(8,128)(2,1)S(1)}, bf16[8,8,2432]{2,1,0:T(8,128)(2,1)S(1)}, u32[]{:S(2)}, u32[]{:S(2)}) collective-permute-start(bf16[8,8,2432]{2,1,0:T(8,128)(2,1)S(1)} %get-tuple-element.40), channel_id=1, source_target_pairs={{0,40},{4,44},{8,48},{12,52},{16,56},{20,60},{24,0},{28,4},{32,8},... | collective-permute-start | bytes 933896 | tf_op jit(solution)/shard_map/ppermute | solution.py:98
  38.0 0.6 dynamic_slice.6
  38.7 6.5 %collective-permute-start.14 = (bf16[5,8,2432]{2,1,0:T(8,128)(2,1)S(1)}, bf16[5,8,2432]{2,1,0:T(8,128)(2,1)S(1)}, u32[]{:S(2)}, u32[]{:S(2)}) collective-permute-start(bf16[5,8,2432]{2,1,0:T(8,128)(2,1)S(1)} %get-tuple-element.47), channel_id=1, source_target_pairs={{0,4},{4,0},{8,12},{12,8},{16,20},{20,16},{24,28},{28,24},{32,36},... | collective-permute-start | bytes 583688 | tf_op jit(solution)/shard_map/ppermute | solution.py:98
  45.2 0.7 fusion
  45.9 1.5 %collective-permute-done.7.refs_0_ = bf16[8,8,2432]{2,1,0:T(8,128)(2,1)S(1)} collective-permute-done((bf16[8,8,2432]{2,1,0:T(8,128)(2,1)}, bf16[8,8,2432]{2,1,0:T(8,128)(2,1)S(1)}, u32[]{:S(2)}, u32[]{:S(2)}) %collective-permute-start.7) | collective-permute-done | bytes 311328 | tf_op jit(solution)/shard_map/ppermute | solution.py:98
  47.4 2.6 %collective-permute-start.16 = (bf16[5,8,2432]{2,1,0:T(8,128)(2,1)S(1)}, bf16[5,8,2432]{2,1,0:T(8,128)(2,1)S(1)}, u32[]{:S(2)}, u32[]{:S(2)}) collective-permute-start(bf16[5,8,2432]{2,1,0:T(8,128)(2,1)S(1)} %get-tuple-element.49), channel_id=1, source_target_pairs={{0,68},{4,64},{8,76},{12,72},{16,84},{20,80},{24,92},{28,88},{32,1... | collective-permute-start | bytes 583688 | tf_op jit(solution)/shard_map/ppermute | solution.py:98
  50.0 23.2 %collective-permute-done.8.refs_1_ = bf16[8,8,2432]{2,1,0:T(8,128)(2,1)S(1)} collective-permute-done((bf16[8,8,2432]{2,1,0:T(8,128)(2,1)}, bf16[8,8,2432]{2,1,0:T(8,128)(2,1)S(1)}, u32[]{:S(2)}, u32[]{:S(2)}) %collective-permute-start.8) | collective-permute-done | bytes 311328 | tf_op jit(solution)/shard_map/ppermute | solution.py:98
  73.2 1.8 %collective-permute-start.17 = (bf16[5,8,2432]{2,1,0:T(8,128)(2,1)S(1)}, bf16[5,8,2432]{2,1,0:T(8,128)(2,1)S(1)}, u32[]{:S(2)}, u32[]{:S(2)}) collective-permute-start(bf16[5,8,2432]{2,1,0:T(8,128)(2,1)S(1)} %get-tuple-element.50), channel_id=1, source_target_pairs={{0,128},{4,132},{8,136},{12,140},{16,144},{20,148},{24,152},{28,15... | collective-permute-start | bytes 583688 | tf_op jit(solution)/shard_map/ppermute | solution.py:98
  75.0 2.2 %collective-permute-start.18 = (bf16[5,8,2432]{2,1,0:T(8,128)(2,1)S(1)}, bf16[5,8,2432]{2,1,0:T(8,128)(2,1)S(1)}, u32[]{:S(2)}, u32[]{:S(2)}) collective-permute-start(bf16[5,8,2432]{2,1,0:T(8,128)(2,1)S(1)} %get-tuple-element.51), channel_id=1, source_target_pairs={{0,132},{4,128},{8,140},{12,136},{16,148},{20,144},{24,156},{28,15... | collective-permute-start | bytes 583688 | tf_op jit(solution)/shard_map/ppermute | solution.py:98
  77.3 1.7 %collective-permute-start.19 = (bf16[5,8,2432]{2,1,0:T(8,128)(2,1)S(1)}, bf16[5,8,2432]{2,1,0:T(8,128)(2,1)S(1)}, u32[]{:S(2)}, u32[]{:S(2)}) collective-permute-start(bf16[5,8,2432]{2,1,0:T(8,128)(2,1)S(1)} %get-tuple-element.52), channel_id=1, source_target_pairs={{0,192},{4,196},{8,200},{12,204},{16,208},{20,212},{24,216},{28,22... | collective-permute-start | bytes 583688 | tf_op jit(solution)/shard_map/ppermute | solution.py:98
  79.0 1.2 %collective-permute-done.17.refs_7_ = bf16[5,8,2432]{2,1,0:T(8,128)(2,1)S(1)} collective-permute-done((bf16[5,8,2432]{2,1,0:T(8,128)(2,1)S(1)}, bf16[5,8,2432]{2,1,0:T(8,128)(2,1)S(1)}, u32[]{:S(2)}, u32[]{:S(2)}) %collective-permute-start.17) | collective-permute-done | bytes 194592 | tf_op jit(solution)/shard_map/ppermute | solution.py:98
  80.2 5.3 %collective-permute-done.18.refs_8_ = bf16[5,8,2432]{2,1,0:T(8,128)(2,1)S(1)} collective-permute-done((bf16[5,8,2432]{2,1,0:T(8,128)(2,1)S(1)}, bf16[5,8,2432]{2,1,0:T(8,128)(2,1)S(1)}, u32[]{:S(2)}, u32[]{:S(2)}) %collective-permute-start.18) | collective-permute-done | bytes 194592 | tf_op jit(solution)/shard_map/ppermute | solution.py:98
  85.4 2.7 %collective-permute-done.19.refs_9_ = bf16[5,8,2432]{2,1,0:T(8,128)(2,1)S(1)} collective-permute-done((bf16[5,8,2432]{2,1,0:T(8,128)(2,1)S(1)}, bf16[5,8,2432]{2,1,0:T(8,128)(2,1)S(1)}, u32[]{:S(2)}, u32[]{:S(2)}) %collective-permute-start.19) | collective-permute-done | bytes 194592 | tf_op jit(solution)/shard_map/ppermute | solution.py:98
  88.2 4.9 %collective-permute-done.20.refs_10_ = bf16[5,8,2432]{2,1,0:T(8,128)(2,1)S(1)} collective-permute-done((bf16[5,8,2432]{2,1,0:T(8,128)(2,1)S(1)}, bf16[5,8,2432]{2,1,0:T(8,128)(2,1)S(1)}, u32[]{:S(2)}, u32[]{:S(2)}) %collective-permute-start.20) | collective-permute-done | bytes 194592 | tf_op jit(solution)/shard_map/ppermute | solution.py:98
  93.1 1.1 %slab.1.a_ref = f32[96,128]{1,0:T(8,128)S(1)} custom-call(bf16[8,8,2432]{2,1,0:T(8,128)(2,1)S(1)} %collective-permute-done.7.refs_0_, bf16[8,8,2432]{2,1,0:T(8,128)(2,1)S(1)} %collective-permute-done.8.refs_1_, bf16[8,8,2432]{2,1,0:T(8,128)(2,1)S(1)} %collective-permute-done.9.refs_2_, bf16[5,8,2432]{2,1,0:T(8,128)(2,1)S(1)} %get-tuple-element.46.refs_3_, ...), custom_call_target="tpu_custom_call" | custom-call | tf_op jit(solution)/shard_map/slab/pallas_call | solution.py:320
  94.2 2.9 %collective-permute-start.21 = (f32[96,128]{1,0:T(8,128)S(1)}, f32[96,128]{1,0:T(8,128)S(1)}, u32[]{:S(2)}, u32[]{:S(2)}) collective-permute-start(f32[96,128]{1,0:T(8,128)S(1)} %slab.1.a_ref), channel_id=1, source_target_pairs={{0,2},{1,3},{2,0},{3,1},{4,6},{5,7},{6,4},{7,5},{8,10},{9,11},{10,... | collective-permute-start | bytes 147464 | tf_op jit(solution)/shard_map/ppermute | solution.py:330
  97.1 0.4 collective-permute-start.22
  97.5 2.3 %collective-permute-start.23 = (f32[96,128]{1,0:T(8,128)S(1)}, f32[96,128]{1,0:T(8,128)S(1)}, u32[]{:S(2)}, u32[]{:S(2)}) collective-permute-start(f32[96,128]{1,0:T(8,128)S(1)} %slab.1.a_ref), channel_id=1, source_target_pairs={{0,3},{1,0},{2,1},{3,2},{4,7},{5,4},{6,5},{7,6},{8,11},{9,8},{10,9... | collective-permute-start | bytes 147464 | tf_op jit(solution)/shard_map/ppermute | solution.py:330
  99.8 1.9 %collective-permute-done.22.c_ref = f32[96,128]{1,0:T(8,128)S(1)} collective-permute-done((f32[96,128]{1,0:T(8,128)S(1)}, f32[96,128]{1,0:T(8,128)S(1)}, u32[]{:S(2)}, u32[]{:S(2)}) %collective-permute-start.22) | collective-permute-done | bytes 49184 | tf_op jit(solution)/shard_map/ppermute | solution.py:330
  101.7 5.6 %solve.1 = (f32[137,1,137]{2,1,0:T(1,128)}, f32[1,137]{1,0:T(1,128)}, f32[1,137]{1,0:T(1,128)}) custom-call(f32[96,128]{1,0:T(8,128)S(1)} %slab.1.a_ref, f32[96,128]{1,0:T(8,128)S(1)} %collective-permute-done.21.b_ref, f32[96,128]{1,0:T(8,128)S(1)} %collective-permute-done.22.c_ref, f32[96,128]{1,0:T(8,128)S(1)} %collective-permute-done.23.d_ref), custom_call_target="tpu_custom_call" | custom-call | tf_op jit(solution)/shard_map/solve/pallas_call | solution.py:334
  (31 shorter events, 1.0 us)
Async XLA Ops:
  0.6 78.3 %copy-start = (f32[64,2176]{1,0:T(8,128)S(1)}, f32[64,2176]{1,0:T(8,128)}, u32[]{:S(2)}) copy-start(f32[64,2176]{1,0:T(8,128)} %param.8) | copy-start | bytes 1671172
  0.6 37.4 %copy-start.2 = (s32[64]{0:T(128)S(1)}, s32[64]{0:T(128)}, u32[]{:S(2)}) copy-start(s32[64]{0:T(128)} %param.9) | copy-start | bytes 772
  0.7 44.6 %copy-start.1 = (f32[2176]{0:T(1024)S(1)}, f32[2176]{0:T(1024)}, u32[]{:S(2)}) copy-start(f32[2176]{0:T(1024)} %param.7) | copy-start | bytes 26116
  3.7 7.5 %collective-permute-start = (bf16[3,8,2432]{2,1,0:T(8,128)(2,1)}, bf16[3,8,2432]{2,1,0:T(8,128)(2,1)S(1)}, u32[]{:S(2)}, u32[]{:S(2)}) collective-permute-start(bf16[3,8,2432]{2,1,0:T(8,128)(2,1)} %get-tuple-element.31), channel_id=1, source_target_pairs={{0,4},{4,0},{8,12},{12,8},{16,20},{20,16},{24,28},{28,24},{32,36},... | collective-permute-start | bytes 350216 | tf_op jit(solution)/shard_map/ppermute | solution.py:98
  7.0 7.2 %collective-permute-start.1 = (bf16[3,8,2432]{2,1,0:T(8,128)(2,1)}, bf16[3,8,2432]{2,1,0:T(8,128)(2,1)S(1)}, u32[]{:S(2)}, u32[]{:S(2)}) collective-permute-start(bf16[3,8,2432]{2,1,0:T(8,128)(2,1)} %get-tuple-element.32), channel_id=1, source_target_pairs={{0,64},{4,68},{8,72},{12,76},{16,80},{20,84},{24,88},{28,92},{32,9... | collective-permute-start | bytes 350216 | tf_op jit(solution)/shard_map/ppermute | solution.py:98
  7.0 14.1 %collective-permute-start.2 = (bf16[3,8,2432]{2,1,0:T(8,128)(2,1)}, bf16[3,8,2432]{2,1,0:T(8,128)(2,1)S(1)}, u32[]{:S(2)}, u32[]{:S(2)}) collective-permute-start(bf16[3,8,2432]{2,1,0:T(8,128)(2,1)} %get-tuple-element.33), channel_id=1, source_target_pairs={{0,68},{4,64},{8,76},{12,72},{16,84},{20,80},{24,92},{28,88},{32,1... | collective-permute-start | bytes 350216 | tf_op jit(solution)/shard_map/ppermute | solution.py:98
  8.0 13.2 %collective-permute-start.3 = (bf16[3,8,2432]{2,1,0:T(8,128)(2,1)}, bf16[3,8,2432]{2,1,0:T(8,128)(2,1)S(1)}, u32[]{:S(2)}, u32[]{:S(2)}) collective-permute-start(bf16[3,8,2432]{2,1,0:T(8,128)(2,1)} %get-tuple-element.34), channel_id=1, source_target_pairs={{0,128},{4,132},{8,136},{12,140},{16,144},{20,148},{24,152},{28,15... | collective-permute-start | bytes 350216 | tf_op jit(solution)/shard_map/ppermute | solution.py:98
  11.1 10.0 %collective-permute-start.4 = (bf16[3,8,2432]{2,1,0:T(8,128)(2,1)}, bf16[3,8,2432]{2,1,0:T(8,128)(2,1)S(1)}, u32[]{:S(2)}, u32[]{:S(2)}) collective-permute-start(bf16[3,8,2432]{2,1,0:T(8,128)(2,1)} %get-tuple-element.35), channel_id=1, source_target_pairs={{0,132},{4,128},{8,140},{12,136},{16,148},{20,144},{24,156},{28,15... | collective-permute-start | bytes 350216 | tf_op jit(solution)/shard_map/ppermute | solution.py:98
  11.2 22.3 %collective-permute-start.10 = (bf16[8,8,2432]{2,1,0:T(8,128)(2,1)}, bf16[8,8,2432]{2,1,0:T(8,128)(2,1)S(1)}, u32[]{:S(2)}, u32[]{:S(2)}) collective-permute-start(bf16[8,8,2432]{2,1,0:T(8,128)(2,1)} %get-tuple-element.41), channel_id=1, source_target_pairs={{0,16},{4,20},{8,24},{12,28},{16,32},{20,36},{24,40},{28,44},{32,4... | collective-permute-start | bytes 933896 | tf_op jit(solution)/shard_map/ppermute | solution.py:98
  14.2 21.8 %collective-permute-start.11 = (bf16[8,8,2432]{2,1,0:T(8,128)(2,1)}, bf16[8,8,2432]{2,1,0:T(8,128)(2,1)S(1)}, u32[]{:S(2)}, u32[]{:S(2)}) collective-permute-start(bf16[8,8,2432]{2,1,0:T(8,128)(2,1)} %get-tuple-element.42), channel_id=1, source_target_pairs={{0,48},{4,52},{8,56},{12,60},{16,0},{20,4},{24,8},{28,12},{32,16},... | collective-permute-start | bytes 933896 | tf_op jit(solution)/shard_map/ppermute | solution.py:98
  21.1 5.1 %collective-permute-start.5 = (bf16[3,8,2432]{2,1,0:T(8,128)(2,1)}, bf16[3,8,2432]{2,1,0:T(8,128)(2,1)S(1)}, u32[]{:S(2)}, u32[]{:S(2)}) collective-permute-start(bf16[3,8,2432]{2,1,0:T(8,128)(2,1)} %get-tuple-element.36), channel_id=1, source_target_pairs={{0,192},{4,196},{8,200},{12,204},{16,208},{20,212},{24,216},{28,22... | collective-permute-start | bytes 350216 | tf_op jit(solution)/shard_map/ppermute | solution.py:98
  21.1 17.5 %collective-permute-start.12 = (bf16[8,8,2432]{2,1,0:T(8,128)(2,1)}, bf16[8,8,2432]{2,1,0:T(8,128)(2,1)S(1)}, u32[]{:S(2)}, u32[]{:S(2)}) collective-permute-start(bf16[8,8,2432]{2,1,0:T(8,128)(2,1)} %get-tuple-element.43), channel_id=1, source_target_pairs={{0,8},{4,12},{8,16},{12,20},{16,24},{20,28},{24,32},{28,36},{32,40... | collective-permute-start | bytes 933896 | tf_op jit(solution)/shard_map/ppermute | solution.py:98
  21.2 17.5 %collective-permute-start.13 = (bf16[8,8,2432]{2,1,0:T(8,128)(2,1)}, bf16[8,8,2432]{2,1,0:T(8,128)(2,1)S(1)}, u32[]{:S(2)}, u32[]{:S(2)}) collective-permute-start(bf16[8,8,2432]{2,1,0:T(8,128)(2,1)} %get-tuple-element.44), channel_id=1, source_target_pairs={{0,56},{4,60},{8,0},{12,4},{16,8},{20,12},{24,16},{28,20},{32,24},... | collective-permute-start | bytes 933896 | tf_op jit(solution)/shard_map/ppermute | solution.py:98
  26.3 6.0 %collective-permute-start.6 = (bf16[3,8,2432]{2,1,0:T(8,128)(2,1)}, bf16[3,8,2432]{2,1,0:T(8,128)(2,1)S(1)}, u32[]{:S(2)}, u32[]{:S(2)}) collective-permute-start(bf16[3,8,2432]{2,1,0:T(8,128)(2,1)} %get-tuple-element.37), channel_id=1, source_target_pairs={{0,196},{4,192},{8,204},{12,200},{16,212},{20,208},{24,220},{28,21... | collective-permute-start | bytes 350216 | tf_op jit(solution)/shard_map/ppermute | solution.py:98
  33.2 14.2 %collective-permute-start.7 = (bf16[8,8,2432]{2,1,0:T(8,128)(2,1)}, bf16[8,8,2432]{2,1,0:T(8,128)(2,1)S(1)}, u32[]{:S(2)}, u32[]{:S(2)}) collective-permute-start(bf16[8,8,2432]{2,1,0:T(8,128)(2,1)} %get-tuple-element.38), channel_id=1, source_target_pairs={{0,32},{4,36},{8,40},{12,44},{16,48},{20,52},{24,56},{28,60},{32,0... | collective-permute-start | bytes 933896 | tf_op jit(solution)/shard_map/ppermute | solution.py:98
  33.6 39.6 %collective-permute-start.8 = (bf16[8,8,2432]{2,1,0:T(8,128)(2,1)}, bf16[8,8,2432]{2,1,0:T(8,128)(2,1)S(1)}, u32[]{:S(2)}, u32[]{:S(2)}) collective-permute-start(bf16[8,8,2432]{2,1,0:T(8,128)(2,1)} %get-tuple-element.39), channel_id=1, source_target_pairs={{0,24},{4,28},{8,32},{12,36},{16,40},{20,44},{24,48},{28,52},{32,5... | collective-permute-start | bytes 933896 | tf_op jit(solution)/shard_map/ppermute | solution.py:98
  36.1 39.0 %collective-permute-start.9 = (bf16[8,8,2432]{2,1,0:T(8,128)(2,1)S(1)}, bf16[8,8,2432]{2,1,0:T(8,128)(2,1)S(1)}, u32[]{:S(2)}, u32[]{:S(2)}) collective-permute-start(bf16[8,8,2432]{2,1,0:T(8,128)(2,1)S(1)} %get-tuple-element.40), channel_id=1, source_target_pairs={{0,40},{4,44},{8,48},{12,52},{16,56},{20,60},{24,0},{28,4},{32,8},... | collective-permute-start | bytes 933896 | tf_op jit(solution)/shard_map/ppermute | solution.py:98
  38.7 38.5 %collective-permute-start.14 = (bf16[5,8,2432]{2,1,0:T(8,128)(2,1)S(1)}, bf16[5,8,2432]{2,1,0:T(8,128)(2,1)S(1)}, u32[]{:S(2)}, u32[]{:S(2)}) collective-permute-start(bf16[5,8,2432]{2,1,0:T(8,128)(2,1)S(1)} %get-tuple-element.47), channel_id=1, source_target_pairs={{0,4},{4,0},{8,12},{12,8},{16,20},{20,16},{24,28},{28,24},{32,36},... | collective-permute-start | bytes 583688 | tf_op jit(solution)/shard_map/ppermute | solution.py:98
  45.2 33.7 %collective-permute-start.15 = (bf16[5,8,2432]{2,1,0:T(8,128)(2,1)S(1)}, bf16[5,8,2432]{2,1,0:T(8,128)(2,1)S(1)}, u32[]{:S(2)}, u32[]{:S(2)}) collective-permute-start(bf16[5,8,2432]{2,1,0:T(8,128)(2,1)S(1)} %get-tuple-element.48), channel_id=1, source_target_pairs={{0,64},{4,68},{8,72},{12,76},{16,80},{20,84},{24,88},{28,92},{32,9... | collective-permute-start | bytes 583688 | tf_op jit(solution)/shard_map/ppermute | solution.py:98
  47.4 31.6 %collective-permute-start.16 = (bf16[5,8,2432]{2,1,0:T(8,128)(2,1)S(1)}, bf16[5,8,2432]{2,1,0:T(8,128)(2,1)S(1)}, u32[]{:S(2)}, u32[]{:S(2)}) collective-permute-start(bf16[5,8,2432]{2,1,0:T(8,128)(2,1)S(1)} %get-tuple-element.49), channel_id=1, source_target_pairs={{0,68},{4,64},{8,76},{12,72},{16,84},{20,80},{24,92},{28,88},{32,1... | collective-permute-start | bytes 583688 | tf_op jit(solution)/shard_map/ppermute | solution.py:98
  73.2 7.0 %collective-permute-start.17 = (bf16[5,8,2432]{2,1,0:T(8,128)(2,1)S(1)}, bf16[5,8,2432]{2,1,0:T(8,128)(2,1)S(1)}, u32[]{:S(2)}, u32[]{:S(2)}) collective-permute-start(bf16[5,8,2432]{2,1,0:T(8,128)(2,1)S(1)} %get-tuple-element.50), channel_id=1, source_target_pairs={{0,128},{4,132},{8,136},{12,140},{16,144},{20,148},{24,152},{28,15... | collective-permute-start | bytes 583688 | tf_op jit(solution)/shard_map/ppermute | solution.py:98
  75.0 10.4 %collective-permute-start.18 = (bf16[5,8,2432]{2,1,0:T(8,128)(2,1)S(1)}, bf16[5,8,2432]{2,1,0:T(8,128)(2,1)S(1)}, u32[]{:S(2)}, u32[]{:S(2)}) collective-permute-start(bf16[5,8,2432]{2,1,0:T(8,128)(2,1)S(1)} %get-tuple-element.51), channel_id=1, source_target_pairs={{0,132},{4,128},{8,140},{12,136},{16,148},{20,144},{24,156},{28,15... | collective-permute-start | bytes 583688 | tf_op jit(solution)/shard_map/ppermute | solution.py:98
  77.3 10.9 %collective-permute-start.19 = (bf16[5,8,2432]{2,1,0:T(8,128)(2,1)S(1)}, bf16[5,8,2432]{2,1,0:T(8,128)(2,1)S(1)}, u32[]{:S(2)}, u32[]{:S(2)}) collective-permute-start(bf16[5,8,2432]{2,1,0:T(8,128)(2,1)S(1)} %get-tuple-element.52), channel_id=1, source_target_pairs={{0,192},{4,196},{8,200},{12,204},{16,208},{20,212},{24,216},{28,22... | collective-permute-start | bytes 583688 | tf_op jit(solution)/shard_map/ppermute | solution.py:98
  78.9 14.1 %collective-permute-start.20 = (bf16[5,8,2432]{2,1,0:T(8,128)(2,1)S(1)}, bf16[5,8,2432]{2,1,0:T(8,128)(2,1)S(1)}, u32[]{:S(2)}, u32[]{:S(2)}) collective-permute-start(bf16[5,8,2432]{2,1,0:T(8,128)(2,1)S(1)} %get-tuple-element.53), channel_id=1, source_target_pairs={{0,196},{4,192},{8,204},{12,200},{16,212},{20,208},{24,220},{28,21... | collective-permute-start | bytes 583688 | tf_op jit(solution)/shard_map/ppermute | solution.py:98
  94.2 5.6 %collective-permute-start.21 = (f32[96,128]{1,0:T(8,128)S(1)}, f32[96,128]{1,0:T(8,128)S(1)}, u32[]{:S(2)}, u32[]{:S(2)}) collective-permute-start(f32[96,128]{1,0:T(8,128)S(1)} %slab.1.a_ref), channel_id=1, source_target_pairs={{0,2},{1,3},{2,0},{3,1},{4,6},{5,7},{6,4},{7,5},{8,10},{9,11},{10,... | collective-permute-start | bytes 147464 | tf_op jit(solution)/shard_map/ppermute | solution.py:330
  97.1 4.6 %collective-permute-start.22 = (f32[96,128]{1,0:T(8,128)S(1)}, f32[96,128]{1,0:T(8,128)S(1)}, u32[]{:S(2)}, u32[]{:S(2)}) collective-permute-start(f32[96,128]{1,0:T(8,128)S(1)} %slab.1.a_ref), channel_id=1, source_target_pairs={{0,1},{1,2},{2,3},{3,0},{4,5},{5,6},{6,7},{7,4},{8,9},{9,10},{10,1... | collective-permute-start | bytes 147464 | tf_op jit(solution)/shard_map/ppermute | solution.py:330
  97.5 4.2 %collective-permute-start.23 = (f32[96,128]{1,0:T(8,128)S(1)}, f32[96,128]{1,0:T(8,128)S(1)}, u32[]{:S(2)}, u32[]{:S(2)}) collective-permute-start(f32[96,128]{1,0:T(8,128)S(1)} %slab.1.a_ref), channel_id=1, source_target_pairs={{0,3},{1,0},{2,1},{3,2},{4,7},{5,4},{6,5},{7,6},{8,11},{9,8},{10,9... | collective-permute-start | bytes 147464 | tf_op jit(solution)/shard_map/ppermute | solution.py:330
